TPU v7x, 256 devices: a whole 4x4x8 slice. The times are simulated.
256 devices in a mesh: rep: 32 (over y_lo, z, core), tp: 8 (over x, y_hi).
Axes of the slice: x: 4, y: 4 (y_hi: 2, y_lo: 2; y = y_hi * 2 + y_lo), z: 8, core: 2. Of those that a mesh axis runs over, the one named last changes fastest.
Arguments:
- activations: bfloat16 [16384, 6144], P('rep', 'tp'), may hold values from -6 to 6
- norm_gain: float32 [6144], replicated, may hold values from 0.5 to 1.5
- query_gain: float32 [128], replicated, may hold values from 0.5 to 18
- key_gain: float32 [128], replicated, may hold values from 0.5 to 18
- project_in: bfloat16 [6144, 24, 384], P('rep', 'tp'), may hold values from -1 to 1
- project_out: bfloat16 [6144, 3072], P('rep', 'tp'), may hold values from -1 to 1
Outputs:
- attended: bfloat16 [16384, 6144], P('rep', 'tp')
- weight_norms: float32 [2], replicated
All inputs are finite; a program needn't handle non-finite values.
Results may differ from a plain program's by a relative error of at most 0.018.
The roundings to bfloat16 on the way count: a program that leaves them out, or rounds other values in their place, can miss the bound.
Values may be sent and summed in bfloat16 or wider, within the bound.
A program may use at most 128 MiB of HBM per device.

v0:
```python
import math

import jax
import jax.numpy as jnp
from jax import lax
from jax.sharding import Mesh
from jax.sharding import PartitionSpec as P

D = 6144
HEADS = 24
HEAD_DIM = 128
PATCHES = 256
TP = ("tp_0", "tp_1")
REP = ("rep_0", "rep_1", "rep_2")
REP_TP = ("rep_0", "rep_1", "rep_2", "tp_0", "tp_1")


def by_axis(array, axes):
    for axis in axes:
        array = lax.psum(array, axis)
    return array


def layer_norm(values, gain):
    average = jnp.mean(values, -1, keepdims=True)
    centred = values - average
    variance = jnp.mean(centred * centred, -1, keepdims=True)
    return centred * lax.rsqrt(variance + 1e-06) * gain


def shards(activations, norm_gain, query_gain, key_gain, project_in, project_out):
    gathered_rows = lax.all_gather(activations, TP, axis=1, tiled=True)
    normed = layer_norm(gathered_rows.astype(jnp.float32), norm_gain).astype(jnp.bfloat16)
    tok_rows = normed.shape[0]
    local_heads = project_in.shape[1]
    head_dim = project_in.shape[2] // 3
    piece = lax.all_gather(project_in, REP, axis=0, tiled=True)
    running = jnp.dot(normed, piece.reshape(piece.shape[0], -1), preferred_element_type=jnp.float32)
    projected = running
    images_here = tok_rows // PATCHES
    projected = projected.reshape(images_here, PATCHES, local_heads, 3 * head_dim)
    queries = layer_norm(projected[..., :head_dim], query_gain).astype(jnp.bfloat16)
    keys_normed = layer_norm(projected[..., head_dim : 2 * head_dim], key_gain).astype(jnp.bfloat16)
    values = projected[..., 2 * head_dim :].astype(jnp.bfloat16)
    scores = jnp.einsum(
        "iphd,iqhd->ihpq", queries, keys_normed, preferred_element_type=jnp.float32
    ) / math.sqrt(head_dim)
    probabilities = jax.nn.softmax(scores, axis=-1).astype(jnp.bfloat16)
    mixed = jnp.einsum("ihpq,iqhd->iphd", probabilities, values, preferred_element_type=jnp.float32)
    mixed = mixed.astype(jnp.bfloat16).reshape(tok_rows, local_heads * head_dim)
    product = lax.dot_general(
        mixed,
        lax.all_gather(project_out, REP, axis=0, tiled=True),
        (((1,), (1,)), ((), ())),
        preferred_element_type=jnp.float32,
    )
    attended = lax.psum_scatter(product.astype(jnp.bfloat16), TP, scatter_dimension=1, tiled=True)
    local_in = jnp.sum(jnp.square(project_in.astype(jnp.float32)))
    local_out = jnp.sum(jnp.square(project_out.astype(jnp.float32)))
    total_in, total_out = (by_axis(local_in, REP_TP), by_axis(local_out, REP_TP))
    weight_norms = jnp.stack([jnp.sqrt(total_in / (3 * HEADS * HEAD_DIM)), jnp.sqrt(total_out / D)])
    return (attended, weight_norms)


def solution(mesh):
    split = Mesh(mesh.devices.reshape(2, 8, 2, 4, 2), ("rep_0", "rep_1", "rep_2", "tp_0", "tp_1"))
    return jax.shard_map(
        shards,
        mesh=split,
        in_specs=(P(REP, TP), P(), P(), P(), P(REP, TP, None), P(REP, TP)),
        out_specs=(P(REP, TP), P()),
        check_vma=False,
    )
```

profile of v0, /device:TPU:32, one launch (start us, length us, event | category | flops | bytes accessed | tf_op | source)
XLA Modules:
  0.0 381.4 jit_solution(14916058992241340326)
XLA Ops:
  7.2 0.0 all-gather.4.cloned.1.call-start
  7.2 0.7 all-gather.4.cloned.1.call-update
  7.9 0.0 all-gather.6.cloned.1.call-start
  7.9 0.7 all-gather.6.cloned.1.call-update
  8.6 0.0 all-gather.8.cloned.1.call-start
  8.7 0.7 all-gather.8.cloned.1.call-update
  9.4 0.0 reduce-scatter.2.cloned.1.call-start
  9.4 97.6 %all-gather.4.cloned.1.call-done = bf16[512,6144]{1,0:T(8,128)(2,1)} async-done(((bf16[512,768]{1,0:T(8,128)(2,1)}), bf16[512,6144]{1,0:T(8,128)(2,1)}) %all-gather.4.cloned.1.call-update) | async-done | bytes 6291472 | tf_op jit(solution)/shard_map/all_gather | solution.py:32
  107.0 0.0 copy-start
  107.0 3.8 %convert_reduce_fusion = f32[512]{0:T(512)S(1)} fusion(bf16[512,6144]{1,0:T(8,128)(2,1)} %all-gather.4.cloned.1.call-done), kind=kLoop, calls=%fused_computation.2 | loop fusion | flops 6290944 | bytes 6293504 | tf_op jit(solution)/shard_map/reduce_sum | solution.py:25
  110.8 0.0 copy-start.4
  110.9 0.7 copy-done
  111.6 1.8 fusion.5
  113.4 0.0 copy-done.4
  113.4 6.2 %fusion.7 = bf16[512,6144]{1,0:T(8,128)(2,1)} fusion(bf16[512,6144]{1,0:T(8,128)(2,1)S(1)} %copy-done, f32[6144]{0:T(1024)S(1)} %copy-done.4, f32[512]{0:T(512)S(1)} %add_rsqrt_fusion.2, f32[512]{0:T(512)S(1)} %broadcast_multiply_fusion.2), kind=kLoop, calls=%fused_computation.9 | loop fusion | flops 15728640 | bytes 12611584 | tf_op jit(solution)/shard_map/convert_element_type | solution.py:33
  119.6 74.2 %all-gather.6.cloned.1.call-done = bf16[6144,3,384]{2,0,1:T(8,128)(2,1)} async-done(((bf16[192,3,384]{2,0,1:T(8,128)(2,1)}), bf16[6144,3,384]{2,0,1:T(8,128)(2,1)}) %all-gather.6.cloned.1.call-update) | async-done | bytes 14155792 | tf_op jit(solution)/shard_map/all_gather | solution.py:37
  193.8 18.7 %copy.14 = bf16[6144,3,384]{0,2,1:T(8,128)(2,1)} copy(bf16[6144,3,384]{2,0,1:T(8,128)(2,1)} %all-gather.6.cloned.1.call-done) | data formatting | bytes 28311552 | tf_op jit(solution)/shard_map/all_gather | solution.py:37
  212.5 0.0 copy-start.5
  212.5 0.0 copy-start.6
  212.5 12.6 %fusion.3 = f32[2,256,3,384]{3,1,2,0:T(8,128)S(1)} fusion(bf16[2,256,6144,1]{2,1,3,0:T(8,128)(2,1)} %bitcast.28, bf16[6144,3,384]{0,2,1:T(8,128)(2,1)} %copy.14), kind=kOutput, calls=%fused_computation.5 | convolution fusion | flops 7247757312 | bytes 22806528 | tf_op jit(solution)/shard_map/dot_general | solution.py:38
  225.2 0.5 slice_reduce_fusion.1
  225.7 0.9 multiply_reduce_fusion.2
  226.6 0.0 copy-done.5
  226.6 0.0 copy-done.6
  226.7 1.0 convolution_multiply_fusion
  227.7 0.0 copy-start.1
  227.7 1.1 copy-done.1
  228.8 0.3 fusion.18
  229.2 2.5 fusion.10
  231.6 0.4 copy.17
  232.1 0.1 copy.21
  232.1 30.1 %all-gather.8.cloned.1.call-done = bf16[6144,384]{1,0:T(8,128)(2,1)} async-done(((bf16[192,384]{1,0:T(8,128)(2,1)}), bf16[6144,384]{1,0:T(8,128)(2,1)}) %all-gather.8.cloned.1.call-update) | async-done | bytes 4718608 | tf_op jit(solution)/shard_map/all_gather | solution.py:53
  262.2 7.8 %convolution_convert_fusion = bf16[512,6144]{1,0:T(8,128)(2,1)} fusion(bf16[512,384]{0,1:T(8,128)(2,1)S(1)} %bitcast.30, bf16[6144,384]{1,0:T(8,128)(2,1)} %all-gather.8.cloned.1.call-done), kind=kOutput, calls=%fused_computation.10 | convolution fusion | flops 2419064832 | bytes 11403264 | tf_op jit(solution)/shard_map/dot_general | solution.py:51
  270.0 0.0 copy-start.2
  270.0 0.0 copy-start.3
  270.0 0.0 reduce-scatter.2.cloned.1.call-update
  270.0 1.0 copy-done.2
  271.0 0.9 multiply_reduce_fusion
  271.8 0.0 copy-done.3
  271.8 0.7 multiply_reduce_fusion.3
  272.5 5.6 %all-reduce.4 = (f32[]{:T(128)}, f32[]{:T(128)}) all-reduce(f32[]{:T(128)} %multiply_reduce_fusion.3, f32[]{:T(128)} %multiply_reduce_fusion), channel_id=1, replica_groups=mesh['rep_0'=2,'rep_1'=8,'rep_2'=2,'tp_0'=4,'tp_1'=2] {'rep_0'}, use_global_device_ids=true, to_apply=%region_16.0 | all-reduce | flops 2 | bytes 16 | tf_op jit(solution)/shard_map/psum | solution.py:20
  278.1 16.2 %all-reduce = (f32[]{:T(128)}, f32[]{:T(128)}) all-reduce(f32[]{:T(128)} %get-tuple-element.14, f32[]{:T(128)} %get-tuple-element.15), channel_id=1, replica_groups=mesh['rep_0'=2,'rep_1'=8,'rep_2'=2,'tp_0'=4,'tp_1'=2] {'rep_1'}, use_global_device_ids=true, to_apply=%region_17.0 | all-reduce | flops 2 | bytes 16 | tf_op jit(solution)/shard_map/psum | solution.py:20
  294.3 3.1 all-reduce.3
  297.4 11.2 %all-reduce.1 = (f32[]{:T(128)}, f32[]{:T(128)}) all-reduce(f32[]{:T(128)} %get-tuple-element.12, f32[]{:T(128)} %get-tuple-element.13), channel_id=1, replica_groups=mesh['rep_0'=2,'rep_1'=8,'rep_2'=2,'tp_0'=4,'tp_1'=2] {'tp_0'}, use_global_device_ids=true, to_apply=%region_19.0 | all-reduce | flops 2 | bytes 16 | tf_op jit(solution)/shard_map/psum | solution.py:20
  308.6 7.1 %all-reduce.2 = (f32[]{:T(128)}, f32[]{:T(128)}) all-reduce(f32[]{:T(128)} %get-tuple-element.8, f32[]{:T(128)} %get-tuple-element.9), channel_id=1, replica_groups=mesh['rep_0'=2,'rep_1'=8,'rep_2'=2,'tp_0'=4,'tp_1'=2] {'tp_1'}, use_global_device_ids=true, to_apply=%region_20.0 | all-reduce | flops 2 | bytes 16 | tf_op jit(solution)/shard_map/psum | solution.py:20
  317.0 0.6 pad_maximum_fusion
  317.6 57.3 %reduce-scatter.2.cloned.1.call-done = bf16[512,768]{1,0:T(8,128)(2,1)} async-done(((bf16[512,6144]{1,0:T(8,128)(2,1)}), bf16[512,768]{1,0:T(8,128)(2,1)}) %reduce-scatter.2.cloned.1.call-update) | async-done | bytes 786448 | tf_op jit(solution)/shard_map/reduce_scatter | solution.py:57
  (5 shorter events, 0.0 us)
Async XLA Ops:
  7.2 99.8 %all-gather.4.cloned.1.call-start = ((), (), s32[]{:S(2)}) async-start(), calls=%async_computation.1 | async-start | bytes 7077888 | tf_op jit(solution)/shard_map/all_gather | solution.py:32
  7.9 185.9 %all-gather.6.cloned.1.call-start = ((), (), s32[]{:S(2)}) async-start(), calls=%async_computation.2 | async-start | bytes 14598144 | tf_op jit(solution)/shard_map/all_gather | solution.py:37
  8.6 253.5 %all-gather.8.cloned.1.call-start = ((), (), s32[]{:S(2)}) async-start(), calls=%async_computation.3 | async-start | bytes 4866048 | tf_op jit(solution)/shard_map/all_gather | solution.py:53
  9.4 365.5 %reduce-scatter.2.cloned.1.call-start = ((), (), s32[]{:S(2)}) async-start(), calls=%async_computation.4 | async-start | bytes 7077888 | tf_op jit(solution)/shard_map/reduce_scatter | solution.py:57
  107.0 4.6 %copy-start = (bf16[512,6144]{1,0:T(8,128)(2,1)S(1)}, bf16[512,6144]{1,0:T(8,128)(2,1)}, u32[]{:S(2)}) copy-start(bf16[512,6144]{1,0:T(8,128)(2,1)} %all-gather.4.cloned.1.call-done) | copy-start | bytes 18874372
  110.8 2.5 copy-start.4
  212.5 14.1 %copy-start.5 = (f32[128]{0:T(128)S(1)}, f32[128]{0:T(128)}, u32[]{:S(2)}) copy-start(f32[128]{0:T(128)} %param.9) | copy-start | bytes 1540
  212.5 14.1 %copy-start.6 = (f32[128]{0:T(128)S(1)}, f32[128]{0:T(128)}, u32[]{:S(2)}) copy-start(f32[128]{0:T(128)} %param.8) | copy-start | bytes 1540
  227.7 1.2 copy-start.1
  270.0 1.0 copy-start.2
  270.0 1.9 copy-start.3
Sparse Core Ops, SparseCore 0:
  10.6 96.3 all-gather.3
  108.8 84.9 all-gather.5
  195.7 66.4 all-gather.7
  270.1 104.7 reduce-scatter.1
where the time goes:
time: 382 us; the launch traced here: 381 us
  waiting for transfers between devices  261 us (68%)
  blocking collectives  43.1 us (11%)
  matrix products  23.9 us (6%)
  local copies, waits for them, and re-layouts  22.1 us (6%)
  other arithmetic  15.7 us (4%)
  between operations  15.2 us (4%)
    all_gather x1, waiting for transfers between devices, shards(): gathered_rows = lax.all_gather(activations, TP, axis=1, tiled=True)  97.6 us
    all_gather x1, waiting for transfers between devices, shards(): piece = lax.all_gather(project_in, REP, axis=0, tiled=True)  74.2 us
    reduce_scatter x1, waiting for transfers between devices, shards(): lax.psum_scatter(product.astype(jnp.bfloat16), TP, scatter_dimension=1, t...  57.3 us
    psum x5, blocking collectives, by_axis(): array = lax.psum(array, axis)  43.1 us
    all_gather x1, waiting for transfers between devices, shards(): lax.all_gather(project_out, REP, axis=0, tiled=True)  30.1 us
    all_gather x1, local copies, waits for them, and re-layouts, shards(): piece = lax.all_gather(project_in, REP, axis=0, tiled=True)  18.7 us
    dot_general x1, matrix products, shards(): jnp.dot(normed, piece.reshape(piece.shape[0], -1), preferred_element_type...  12.6 us
    dot_general x1, matrix products, shards(): lax.dot_general(mixed, lax.all_gather(project_out, REP, axis=0, tiled=Tru...  7.8 us
  transfers between devices with their start and end apart: 4, of which 4 were waited for; matrix products, arithmetic and copies ran while one was open for 13% of the time, Pallas kernels for 0%

commit v1 on v0

v1 whole, which is shorter than its diff:
```python
import math

import jax
import jax.numpy as jnp
from jax import lax
from jax.experimental import pallas as pl
from jax.experimental.pallas import tpu as pltpu
from jax.sharding import PartitionSpec as P

D = 6144
HEADS = 24
HEAD_DIM = 128
PATCHES = 256
NX, NZ = 4, 8
MESH = pl.DeviceIdType.MESH
F32, BF16 = jnp.float32, jnp.bfloat16
EPS = 1e-06
NSEM = 160


def dot_nt(a, b):
    return lax.dot_general(a, b, (((1,), (1,)), ((), ())), preferred_element_type=F32)


def kernel(
    x_ref, gain_ref, qg_ref, kg_ref, w_ref, wo_ref, out_ref, norm_ref,
    gi, go, xg, acc, mixed, part, r1, r2, r3, tsum, nown, nrecv,
    send, recv, local,
):
    rep, tp = lax.axis_index("rep"), lax.axis_index("tp")
    c = lax.rem(rep, 2)
    z = lax.rem(lax.div(rep, 2), NZ)
    yl = lax.div(rep, 2 * NZ)
    x, yh = lax.div(tp, 2), lax.rem(tp, 2)

    def rep_of(yl_, z_, c_):
        return (yl_ * NZ + z_) * 2 + c_

    zp, zm = lax.rem(z + 1, NZ), lax.rem(z + NZ - 1, NZ)
    xp, xm = lax.rem(x + 1, NX), lax.rem(x + NX - 1, NX)
    xf = lax.rem(x + 2, NX)
    dev = {
        "z+": (rep_of(yl, zp, c), tp),
        "z-": (rep_of(yl, zm, c), tp),
        "c": (rep_of(yl, z, 1 - c), tp),
        "y": (rep_of(1 - yl, z, c), tp),
        "x+": (rep, xp * 2 + yh),
        "x-": (rep, xm * 2 + yh),
        "h": (rep, x * 2 + 1 - yh),
    }

    barrier = pltpu.get_barrier_semaphore()
    for d in dev.values():
        pl.semaphore_signal(barrier, inc=1, device_id=d, device_id_type=MESH)
    pl.semaphore_wait(barrier, len(dev))

    ids = {}
    started = []

    def ident(name):
        return ids.setdefault(name, len(ids))

    def push(name, src, dst, to):
        k = ident(name)
        copy = pltpu.make_async_remote_copy(
            src_ref=src, dst_ref=dst, send_sem=send.at[k], recv_sem=recv.at[k],
            device_id=dev[to], device_id_type=MESH,
        )
        copy.start()
        started.append((name, copy))

    def take(name, dst):
        k = ident(name)
        pltpu.make_async_remote_copy(
            src_ref=dst, dst_ref=dst, send_sem=send.at[k], recv_sem=recv.at[k],
            device_id=dev["c"], device_id_type=MESH,
        ).wait_recv()

    def sent(prefix):
        for item in [s for s in started if s[0].startswith(prefix)]:
            item[1].wait_send()
            started.remove(item)

    def piece(other, dz, partner=0):
        yl_ = 1 - yl if other else yl
        c_ = 1 - c if partner else c
        return rep_of(yl_, lax.rem(z + dz + NZ, NZ), c_)

    me_r, me_t = piece(0, 0), tp
    push("ah", x_ref, xg.at[me_t], "h")
    push("ax+own", x_ref, xg.at[me_t], "x+")
    push("ax-own", x_ref, xg.at[me_t], "x-")
    push("iz+1own", w_ref, gi.at[me_r], "z+")
    push("iz-1own", w_ref, gi.at[me_r], "z-")
    push("iy0", w_ref, gi.at[me_r], "y")
    push("ic own0", w_ref, gi.at[me_r], "c")
    locals_ = [
        pltpu.make_async_copy(x_ref, xg.at[me_t], local.at[0]),
        pltpu.make_async_copy(w_ref, gi.at[me_r], local.at[1]),
        pltpu.make_async_copy(wo_ref, go.at[me_r], local.at[2]),
    ]
    for copy in locals_:
        copy.start()

    def half(ref, sign):
        rows = ref.shape[0] // 2
        return ref.at[pl.ds(0 if sign == "+" else rows, rows)]

    def opp(sign):
        return 1 if sign == "+" else -1

    def take_z(kind, buf, col, sign, d):
        r = piece(col == "oth", -opp(sign) * d)
        ref = buf.at[r]
        take(kind + "z" + sign + str(d) + col, half(ref, sign) if d == NZ // 2 else ref)

    def push_z(kind, buf, col, sign, d):
        r = piece(col == "oth", -opp(sign) * (d - 1))
        ref = buf.at[r]
        ref = half(ref, sign) if d == NZ // 2 else ref
        push(kind + "z" + sign + str(d) + col, ref, ref, "z" + sign)

    def swap(kind, buf, col, dz):
        ref = buf.at[piece(col == "oth", dz)]
        push(kind + "c " + col + str(dz), ref, ref, "c")

    def cross(kind, buf, dz):
        ref = buf.at[piece(0, dz)]
        push(kind + "y" + str(dz), ref, ref, "y")

    def take_cross(kind, buf, dz):
        take(kind + "y" + str(dz), buf.at[piece(1, dz)])

    def take_swap(kind, buf, col, dz):
        take(kind + "c " + col + str(dz), buf.at[piece(col == "oth", dz, 1)])

    tile = {
        "own+": xm * 2 + yh, "own-": xp * 2 + yh,
        "par+": xm * 2 + 1 - yh, "par-": xp * 2 + 1 - yh,
        "ownf": xf * 2 + yh, "parf": xf * 2 + 1 - yh,
    }

    def acts_step(who):
        for sign in "+-":
            ref = xg.at[tile[who + sign]]
            take("ax" + sign + who, ref)
            push("ax" + sign + who + "f", half(ref, sign), half(ref, sign), "x" + sign)

    def acts_far(who):
        for sign in "+-":
            take("ax" + sign + who + "f", half(xg.at[tile[who + "f"]], sign))

    for sign in "+-":
        take_z("i", gi, "own", sign, 1)
        push_z("i", gi, "own", sign, 2)
        cross("i", gi, -opp(sign))
        swap("i", gi, "own", -opp(sign))
    take_cross("i", gi, 0)
    swap("i", gi, "oth", 0)
    acts_step("own")
    par = xg.at[x * 2 + 1 - yh]
    take("ah", par)
    push("ax+par", par, par, "x+")
    push("ax-par", par, par, "x-")
    for sign in "+-":
        take_z("i", gi, "own", sign, 2)
        push_z("i", gi, "own", sign, 3)
        swap("i", gi, "own", -2 * opp(sign))
    push("oy0", wo_ref, go.at[me_r], "y")
    push("oc own0", wo_ref, go.at[me_r], "c")
    for sign in "+-":
        take_cross("i", gi, -opp(sign))
        push_z("i", gi, "oth", sign, 2)
        swap("i", gi, "oth", -opp(sign))
    for sign in "+-":
        take_z("i", gi, "own", sign, 3)
        push_z("i", gi, "own", sign, 4)
        swap("i", gi, "own", -3 * opp(sign))
    acts_far("own")
    for sign in "+-":
        take_z("i", gi, "oth", sign, 2)
        push_z("i", gi, "oth", sign, 3)
        swap("i", gi, "oth", -2 * opp(sign))
    acts_step("par")
    for sign in "+-":
        take_z("i", gi, "own", sign, 4)
    swap("i", gi, "own", 4)
    for sign in "+-":
        take_z("i", gi, "oth", sign, 3)
        push_z("i", gi, "oth", sign, 4)
        push("oz" + sign + "1own", wo_ref, go.at[me_r], "z" + sign)
        swap("i", gi, "oth", -3 * opp(sign))
    acts_far("par")
    sent("ax")
    sent("ah")
    locals_[0].wait()

    def norm_rows(i, carry):
        rows = pl.ds(pl.multiple_of(i * 32, 32), 32)

        def lanes(v):
            total = v[:, :128]
            for j in range(1, 6):
                total = total + v[:, j * 128:(j + 1) * 128]
            return total

        total = jnp.zeros((32, 128), F32)
        for t in range(8):
            total = total + lanes(xg[t, rows, :].astype(F32))
        mean = jnp.sum(total, -1, keepdims=True) * (1.0 / D)
        total = jnp.zeros((32, 128), F32)
        for t in range(8):
            v = xg[t, rows, :].astype(F32) - mean
            total = total + lanes(v * v)
        scale = lax.rsqrt(jnp.sum(total, -1, keepdims=True) * (1.0 / D) + EPS)
        for t in range(8):
            v = (xg[t, rows, :].astype(F32) - mean) * scale * gain_ref[pl.ds(t, 1), :]
            xg[t, rows, :] = v.astype(BF16)
        return carry

    lax.fori_loop(0, 16, norm_rows, 0)

    for sign in "+-":
        take_z("i", gi, "oth", sign, 4)
    swap("i", gi, "oth", 4)
    for col in ("own", "oth"):
        for dz in (0, 1, -1, 2, -2, 3, -3, 4):
            take_swap("i", gi, col, dz)
    locals_[1].wait()

    def project(k, first):
        def rows_step(m, carry):
            rows = pl.ds(pl.multiple_of(m * 256, 256), 256)
            w = gi[pl.ds(k * 4, 4)].reshape(768, 1152)
            value = jnp.dot(xg[k, rows, :], w, preferred_element_type=F32)
            if first:
                acc[rows, :] = value
            else:
                acc[rows, :] += value
            return carry

        lax.fori_loop(0, 2, rows_step, 0)

    def project_many(lo, hi):
        def step(k, carry):
            project(k, False)
            return carry

        lax.fori_loop(lo, hi, step, 0)

    def out_ring(d):
        for sign in "+-":
            take_z("o", go, "own", sign, d)
            if d < 4:
                push_z("o", go, "own", sign, d + 1)
                cross("o", go, -opp(sign) * d)
                swap("o", go, "own", -opp(sign) * d)
        if d == 4:
            cross("o", go, 4)
            swap("o", go, "own", 4)

    project(0, True)
    out_ring(1)
    project_many(1, 3)
    out_ring(2)
    project_many(3, 5)
    out_ring(3)
    project_many(5, 8)
    out_ring(4)

    def head_norm(v, gain):
        v = v - jnp.mean(v, -1, keepdims=True)
        var = jnp.mean(v * v, -1, keepdims=True)
        return (v * lax.rsqrt(var + EPS) * gain).astype(BF16)

    def attend(i, carry):
        rows = pl.ds(pl.multiple_of(i * PATCHES, PATCHES), PATCHES)
        for h in range(3):
            lo = h * 3 * HEAD_DIM
            q = head_norm(acc[rows, lo:lo + HEAD_DIM], qg_ref[...])
            k = head_norm(acc[rows, lo + HEAD_DIM:lo + 2 * HEAD_DIM], kg_ref[...])
            v = acc[rows, lo + 2 * HEAD_DIM:lo + 3 * HEAD_DIM].astype(BF16)
            s = dot_nt(q, k) / math.sqrt(HEAD_DIM)
            e = jnp.exp(s - jnp.max(s, -1, keepdims=True))
            p = (e / jnp.sum(e, -1, keepdims=True)).astype(BF16)
            o = jnp.dot(p, v, preferred_element_type=F32)
            mixed[rows, h * HEAD_DIM:(h + 1) * HEAD_DIM] = o.astype(BF16)
        return carry

    lax.fori_loop(0, 2, attend, 0)

    for dz in (0, 1, -1, 2, -2, 3, -3, 4):
        take_cross("o", go, dz)
        swap("o", go, "oth", dz)
    for col in ("own", "oth"):
        for dz in (0, 1, -1, 2, -2, 3, -3, 4):
            take_swap("o", go, col, dz)
    locals_[2].wait()

    def out_part(t):
        w = go[pl.ds(t * 4, 4)].reshape(768, 384)
        part[t] = dot_nt(mixed[...], w).astype(BF16)

    a_rows, b_rows = pl.ds(0, 256), pl.ds(256, 256)
    span = {"+": a_rows, "-": b_rows}
    other = {"+": b_rows, "-": a_rows}
    ys = {"p": 1 - yh, "o": yh}
    near = {"+": xp, "-": xm}

    for g in "po":
        t = xf * 2 + ys[g]
        out_part(t)
        for i, sign in enumerate("+-"):
            push("f" + sign + g, part.at[t, span[sign]], r1.at["po".index(g), i], "x" + sign)
    for g in "po":
        for i, sign in enumerate("+-"):
            t = near[sign] * 2 + ys[g]
            out_part(t)
            push("n" + sign + g + "d", part.at[t, other[sign]], r2.at["po".index(g), i, other[sign]], "x" + sign)
        for i, sign in enumerate("+-"):
            t = near[sign] * 2 + ys[g]
            take("f" + sign + g, r1.at["po".index(g), i])
            part[t, span[sign]] = (part[t, span[sign]].astype(F32) + r1["po".index(g), i].astype(F32)).astype(BF16)
            push("n" + sign + g + "s", part.at[t, span[sign]], r2.at["po".index(g), i, span[sign]], "x" + sign)
        out_part(x * 2 + ys[g])

    def squares(ref, r, total):
        v = ref[r].astype(F32)
        v = v * v
        w = v.shape[1]
        row = v[:, :128]
        for j in range(1, w // 128):
            row = row + v[:, j * 128:(j + 1) * 128]
        return total + jnp.sum(row.reshape(24, 8, 128), 0)

    zero = jnp.zeros((8, 128), F32)
    nown[0, pl.ds(0, 8), :] = lax.fori_loop(0, 32, lambda r, t: squares(gi, r, t), zero)
    nown[0, pl.ds(8, 8), :] = lax.fori_loop(0, 32, lambda r, t: squares(go, r, t), zero)

    x1 = x + 1 - 2 * lax.rem(x, 2)
    dev["n0"] = dev["h"]
    dev["n1"] = (rep, x1 * 2 + yh)
    dev["n2"] = (rep, (NX - 1 - x) * 2 + yh)

    def norm_push(s):
        push("norm" + str(s), nown.at[s], nrecv.at[s], "n" + str(s))

    def norm_take(s):
        take("norm" + str(s), nrecv.at[s])
        nown[s + 1] = nown[s] + nrecv[s]

    norm_push(0)

    def take_near(g, rows, sign):
        i = "+-".index(sign)
        kind = "s" if rows is span[sign] else "d"
        take("n" + sign + g + kind, r2.at["po".index(g), i, rows])

    mine = x * 2 + yh
    theirs = x * 2 + 1 - yh
    for sign in "+-":
        take_near("p", other[sign], sign)
    for sign in "+-":
        take_near("p", span[sign], sign)
    for n, rows in enumerate((a_rows, b_rows)):
        total = part[theirs, rows].astype(F32) + r2[0, 0, rows].astype(F32) + r2[0, 1, rows].astype(F32)
        tsum[rows] = total.astype(BF16)
        push("t" + str(n), tsum.at[rows], r3.at[rows], "h")
    norm_take(0)
    norm_push(1)
    for sign in "+-":
        take_near("o", other[sign], sign)
    norm_take(1)
    norm_push(2)
    norm_take(2)
    total_in = jnp.sum(nown[3, pl.ds(0, 8), :], keepdims=True)
    total_out = jnp.sum(nown[3, pl.ds(8, 8), :], keepdims=True)
    norm_ref[pl.ds(0, 1), :] = jnp.broadcast_to(jnp.sqrt(total_in / (3 * HEADS * HEAD_DIM)), (1, 128))
    norm_ref[pl.ds(1, 1), :] = jnp.broadcast_to(jnp.sqrt(total_out / D), (1, 128))
    for n, rows in enumerate((a_rows, b_rows)):
        take("t" + str(n), r3.at[rows])
    for sign in "+-":
        take_near("o", span[sign], sign)
    for rows in (a_rows, b_rows):
        total = part[mine, rows].astype(F32) + r2[1, 0, rows].astype(F32) + r2[1, 1, rows].astype(F32)
        out_ref[rows] = (total + r3[rows].astype(F32)).astype(BF16)
    sent("")
    assert len(ids) <= NSEM


def shards(activations, norm_gain, query_gain, key_gain, project_in, project_out):
    rows, cols = activations.shape
    depth = project_in.shape[0]
    vmem = pl.BlockSpec(memory_space=pltpu.VMEM)
    out, norms = pl.pallas_call(
        kernel,
        name="block",
        out_shape=(jax.ShapeDtypeStruct((rows, cols), BF16), jax.ShapeDtypeStruct((2, 128), F32)),
        in_specs=[vmem] * 6,
        out_specs=(vmem, vmem),
        scratch_shapes=[
            pltpu.VMEM((32, 192, 1152), BF16),
            pltpu.VMEM((32, 192, 384), BF16),
            pltpu.VMEM((8, 512, 768), BF16),
            pltpu.VMEM((512, 1152), F32),
            pltpu.VMEM((512, 384), BF16),
            pltpu.VMEM((8, 512, 768), BF16),
            pltpu.VMEM((2, 2, 256, 768), BF16),
            pltpu.VMEM((2, 2, 512, 768), BF16),
            pltpu.VMEM((512, 768), BF16),
            pltpu.VMEM((512, 768), BF16),
            pltpu.VMEM((4, 16, 128), F32),
            pltpu.VMEM((3, 16, 128), F32),
            pltpu.SemaphoreType.DMA((NSEM,)),
            pltpu.SemaphoreType.DMA((NSEM,)),
            pltpu.SemaphoreType.DMA((3,)),
        ],
        compiler_params=pltpu.CompilerParams(
            collective_id=0, has_side_effects=True, vmem_limit_bytes=63 * 1024 * 1024
        ),
    )(
        activations,
        norm_gain.reshape(8, 768),
        query_gain.reshape(1, HEAD_DIM),
        key_gain.reshape(1, HEAD_DIM),
        project_in.reshape(depth, -1),
        project_out,
    )
    return out, norms[:, 0]


def solution(mesh):
    return jax.shard_map(
        shards,
        mesh=mesh,
        in_specs=(P("rep", "tp"), P(), P(), P(), P("rep", "tp", None), P("rep", "tp")),
        out_specs=(P("rep", "tp"), P()),
        check_vma=False,
    )
```

time: 382 us -> 184 us (0.48)
  waiting for transfers between devices: 261 us -> 0 us
  Pallas kernels: 0 us -> 175 us
  blocking collectives: 43.1 us -> 0 us
  matrix products: 23.9 us -> 0 us
  other arithmetic: 15.7 us -> 0 us
  local copies, waits for them, and re-layouts: 22.1 us -> 6.5 us
  between operations: 15.2 us -> 0.65 us
    all_gather x3 -> x0, waiting for transfers between devices: 202 us -> none  [the longest x1 97.6 us: shards(): gathered_rows = lax.all_gather(activations, TP, axis=1, tiled=True)]
    pallas_call x0 -> x1, Pallas kernels: none -> 175 us  [shards(): pl.pallas_call(kernel, name='block', out_shape=(jax.ShapeDtypeStruct((row...]
    reduce_scatter x1 -> x0, waiting for transfers between devices: 57.3 us -> none  [shards(): lax.psum_scatter(product.astype(jnp.bfloat16), TP, scatter_dimension=1, t...]
    psum x5 -> x0, blocking collectives: 43.1 us -> none  [by_axis(): array = lax.psum(array, axis)]
    dot_general x4 -> x0, matrix products: 23.9 us -> none  [the longest x1 12.6 us: shards(): jnp.dot(normed, piece.reshape(piece.shape[0], -1), preferred_element_type...]
    all_gather x1 -> x0, local copies, waits for them, and re-layouts: 18.7 us -> none  [shards(): piece = lax.all_gather(project_in, REP, axis=0, tiled=True)]
    reduce_sum x6 -> x0, other arithmetic: 8.55 us -> none  [the longest x2 4.33 us: layer_norm(): average = jnp.mean(values, -1, keepdims=True)]
    convert_element_type x1 -> x0, other arithmetic: 6.23 us -> none  [shards(): layer_norm(gathered_rows.astype(jnp.float32), norm_gain)]
  transfers between devices with their start and end apart: 4 -> 0, of which waited for: 4 -> 0; matrix products, arithmetic and copies ran while one was open for 13% -> 0% of each run, Pallas kernels for 0% -> 0%
where the time goes in v1:
time: 184 us; the launch traced here: 182 us
  Pallas kernels  175 us (95%)
  local copies, waits for them, and re-layouts  6.5 us (4%)
    pallas_call x1, Pallas kernels, shards(): pl.pallas_call(kernel, name='block', out_shape=(jax.ShapeDtypeStruct((row...  175 us

profile of v1, /device:TPU:32, one launch (start us, length us, event | category | flops | bytes accessed | tf_op | source)
XLA Modules:
  0.0 182.0 jit_solution(12693261552178636871)
XLA Ops:
  0.6 1.3 reshape.16.gain_ref
  2.0 1.8 copy.10
  3.8 174.9 %block.1 = (bf16[512,768]{1,0:T(8,128)(2,1)}, f32[2,128]{1,0:T(2,128)}) custom-call(bf16[512,768]{1,0:T(8,128)(2,1)} %x_ref.1, f32[8,768]{1,0:T(8,128)} %reshape.16.gain_ref, f32[1,128]{1,0:T(1,128)} %bitcast.6, f32[1,128]{1,0:T(1,128)} %bitcast.7, bf16[192,1152]{1,0:T(8,128)(2,1)} %bitcast.4, bf16[192,384]{1,0:T(8,128)(2,1)} %wo_ref.1), custom_call_target="tpu_custom_call" | custom-call | tf_op jit(solution)/shard_map/block/pallas_call | solution.py:395
  178.7 0.0 copy-start
  178.7 0.6 copy-done
  179.3 0.6 slice_reduce_fusion
  179.9 2.1 %copy.12 = bf16[512,768]{1,0:T(8,128)(2,1)} copy(bf16[512,768]{1,0:T(8,128)(2,1)} %get-tuple-element.8) | data formatting | bytes 1572864
Async XLA Ops:
  178.7 0.7 copy-start

commit v2 on v1

v2 whole, which is shorter than its diff:
```python
import math

import jax
import jax.numpy as jnp
from jax import lax
from jax.experimental import pallas as pl
from jax.experimental.pallas import tpu as pltpu
from jax.sharding import PartitionSpec as P

D = 6144
HEADS = 24
HEAD_DIM = 128
PATCHES = 256
NX, NZ = 4, 8
MESH = pl.DeviceIdType.MESH
F32, BF16 = jnp.float32, jnp.bfloat16
EPS = 1e-06
NSEM = 160


def dot_nt(a, b):
    return lax.dot_general(a, b, (((1,), (1,)), ((), ())), preferred_element_type=F32)


def kernel(
    x_ref, gain_ref, qg_ref, kg_ref, w_ref, wo_ref, out_ref, norm_ref,
    gi, go, xg, acc, mixed, part, r1, r2, r3, r4, tsum, nown, nrecv,
    send, recv, local,
):
    rep, tp = lax.axis_index("rep"), lax.axis_index("tp")
    c = lax.rem(rep, 2)
    z = lax.rem(lax.div(rep, 2), NZ)
    yl = lax.div(rep, 2 * NZ)
    x, yh = lax.div(tp, 2), lax.rem(tp, 2)

    def rep_of(yl_, z_, c_):
        return (yl_ * NZ + z_) * 2 + c_

    zp, zm = lax.rem(z + 1, NZ), lax.rem(z + NZ - 1, NZ)
    xp, xm = lax.rem(x + 1, NX), lax.rem(x + NX - 1, NX)
    xf = lax.rem(x + 2, NX)
    dev = {
        "z+": (rep_of(yl, zp, c), tp),
        "z-": (rep_of(yl, zm, c), tp),
        "c": (rep_of(yl, z, 1 - c), tp),
        "y": (rep_of(1 - yl, z, c), tp),
        "x+": (rep, xp * 2 + yh),
        "x-": (rep, xm * 2 + yh),
        "h": (rep, x * 2 + 1 - yh),
    }

    ids = {}
    started = []

    def ident(name):
        return ids.setdefault(name, len(ids))

    def push(name, src, dst, to):
        k = ident(name)
        copy = pltpu.make_async_remote_copy(
            src_ref=src, dst_ref=dst, send_sem=send.at[k], recv_sem=recv.at[k],
            device_id=dev[to], device_id_type=MESH,
        )
        copy.start()
        started.append((name, copy))

    def take(name, dst):
        k = ident(name)
        pltpu.make_async_remote_copy(
            src_ref=dst, dst_ref=dst, send_sem=send.at[k], recv_sem=recv.at[k],
            device_id=dev["c"], device_id_type=MESH,
        ).wait_recv()

    def sent(prefix):
        for item in [s for s in started if s[0].startswith(prefix)]:
            item[1].wait_send()
            started.remove(item)

    def piece(other, dz, partner=0):
        yl_ = 1 - yl if other else yl
        c_ = 1 - c if partner else c
        return rep_of(yl_, lax.rem(z + dz + NZ, NZ), c_)

    me_r, me_t = piece(0, 0), tp
    own_x, own_w, own_o = xg.at[me_t], gi.at[me_r], go.at[me_r]
    fetch = [pltpu.make_async_copy(x_ref, own_x, local.at[0])]
    for h in range(3):
        fetch.append(pltpu.make_async_copy(w_ref.at[h], own_w.at[:, pl.ds(h * 384, 384)], local.at[1 + h]))
    fetch.append(pltpu.make_async_copy(wo_ref, own_o, local.at[4]))
    for copy in fetch:
        copy.start()

    barrier = pltpu.get_barrier_semaphore()
    for d in dev.values():
        pl.semaphore_signal(barrier, inc=1, device_id=d, device_id_type=MESH)
    pl.semaphore_wait(barrier, len(dev))

    fetch[0].wait()
    push("ah", own_x, own_x, "h")
    push("ax+own", own_x, own_x, "x+")
    push("ax-own", own_x, own_x, "x-")
    for copy in fetch[1:4]:
        copy.wait()
    rows96 = (pl.ds(0, 96), pl.ds(96, 96))
    for n in (0, 1):
        for sign, m in (("+", n), ("-", 1 - n)):
            ref = gi.at[me_r, rows96[m]]
            push("iz" + sign + "1own" + str(m), ref, ref, "z" + sign)
    push("ic own0", own_w, own_w, "c")
    fetch[4].wait()

    def rows_of(ref, n):
        rows = ref.shape[0] // 2
        return ref.at[pl.ds(n * rows, rows)]

    def opp(sign):
        return 1 if sign == "+" else -1

    def lead(sign):
        return 0 if sign == "+" else 1

    def take_z(kind, buf, col, sign, d, n):
        ref = rows_of(buf.at[piece(col == "oth", -opp(sign) * d)], n)
        take(kind + "z" + sign + str(d) + col + str(n), ref)

    def push_z(kind, buf, col, sign, d, n):
        ref = rows_of(buf.at[piece(col == "oth", -opp(sign) * (d - 1))], n)
        push(kind + "z" + sign + str(d) + col + str(n), ref, ref, "z" + sign)

    def swap(kind, buf, col, dz):
        ref = buf.at[piece(col == "oth", dz)]
        push(kind + "c " + col + str(dz), ref, ref, "c")

    def cross(kind, buf, dz):
        ref = buf.at[piece(0, dz)]
        push(kind + "y" + str(dz), ref, ref, "y")

    def take_cross(kind, buf, dz):
        take(kind + "y" + str(dz), buf.at[piece(1, dz)])

    def take_swap(kind, buf, col, dz):
        take(kind + "c " + col + str(dz), buf.at[piece(col == "oth", dz, 1)])

    tile = {
        "own+": xm * 2 + yh, "own-": xp * 2 + yh,
        "par+": xm * 2 + 1 - yh, "par-": xp * 2 + 1 - yh,
        "ownf": xf * 2 + yh, "parf": xf * 2 + 1 - yh,
    }

    def acts_step(who):
        for sign in "+-":
            ref = xg.at[tile[who + sign]]
            take("ax" + sign + who, ref)
            ref = rows_of(ref, lead(sign))
            push("ax" + sign + who + "f", ref, ref, "x" + sign)

    def acts_far(who):
        for sign in "+-":
            take("ax" + sign + who + "f", rows_of(xg.at[tile[who + "f"]], lead(sign)))

    def relay(kind, buf, col, d, which, onward=True):
        for sign in "+-":
            n = lead(sign) if which == "lead" else 1 - lead(sign)
            take_z(kind, buf, col, sign, d, n)
            if onward and (d < 3 or (d == 3 and which == "lead")):
                push_z(kind, buf, col, sign, d + 1, n)

    def swap_both(kind, buf, col, d):
        for sign in "+-":
            swap(kind, buf, col, -opp(sign) * d)

    def whole(kind, buf, d):
        for which in ("lead", "rest"):
            relay(kind, buf, "own", d, which)
        for sign in "+-":
            cross(kind, buf, -opp(sign) * d)
            swap(kind, buf, "own", -opp(sign) * d)

    relay("i", gi, "own", 1, "lead")
    relay("i", gi, "own", 1, "rest")
    for dz in (1, -1):
        cross("i", gi, dz)
        swap("i", gi, "own", dz)
    push("iy0", own_w, own_w, "y")
    push("oy0", own_o, own_o, "y")
    push("oc own0", own_o, own_o, "c")
    for sign in "+-":
        for n in (lead(sign), 1 - lead(sign)):
            push_z("o", go, "own", sign, 1, n)
    relay("i", gi, "own", 2, "lead")
    par = xg.at[x * 2 + 1 - yh]
    take("ah", par)
    push("ax+par", par, par, "x+")
    push("ax-par", par, par, "x-")
    acts_step("own")
    relay("i", gi, "own", 2, "rest")
    swap_both("i", gi, "own", 2)
    relay("i", gi, "own", 3, "lead")
    whole("o", go, 1)
    take_cross("i", gi, 1)
    for n in (1, 0):
        push_z("i", gi, "oth", "-", 2, n)
    swap("i", gi, "oth", 1)
    relay("i", gi, "own", 3, "rest")
    swap_both("i", gi, "own", 3)
    take_cross("i", gi, -1)
    for n in (0, 1):
        push_z("i", gi, "oth", "+", 2, n)
    swap("i", gi, "oth", -1)
    relay("i", gi, "own", 4, "lead", False)
    swap("i", gi, "own", 4)
    acts_step("par")
    whole("o", go, 2)
    acts_far("own")
    relay("i", gi, "oth", 2, "lead")
    take_cross("i", gi, 0)
    swap("i", gi, "oth", 0)
    relay("i", gi, "oth", 2, "rest")
    swap_both("i", gi, "oth", 2)
    whole("o", go, 3)
    acts_far("par")
    sent("ax")
    sent("ah")

    def norm_rows(i, carry):
        rows = pl.ds(pl.multiple_of(i * 32, 32), 32)

        def lanes(v):
            total = v[:, :128]
            for j in range(1, 6):
                total = total + v[:, j * 128:(j + 1) * 128]
            return total

        total = jnp.zeros((32, 128), F32)
        for t in range(8):
            total = total + lanes(xg[t, rows, :].astype(F32))
        mean = jnp.sum(total, -1, keepdims=True) * (1.0 / D)
        total = jnp.zeros((32, 128), F32)
        for t in range(8):
            v = xg[t, rows, :].astype(F32) - mean
            total = total + lanes(v * v)
        scale = lax.rsqrt(jnp.sum(total, -1, keepdims=True) * (1.0 / D) + EPS)
        for t in range(8):
            v = (xg[t, rows, :].astype(F32) - mean) * scale * gain_ref[pl.ds(t * 768, 768)].reshape(1, 768)
            xg[t, rows, :] = v.astype(BF16)
        return carry

    lax.fori_loop(0, 16, norm_rows, 0)

    relay("i", gi, "oth", 3, "lead")
    for dz in (0, 1, -1, 2, -2, 3, -3, 4):
        take_swap("i", gi, "own", dz)

    def project(k, first):
        def rows_step(m, carry):
            rows = pl.ds(pl.multiple_of(m * 256, 256), 256)
            w = gi[pl.ds(k * 4, 4)].reshape(768, 1152)
            value = jnp.dot(xg[k, rows, :], w, preferred_element_type=F32)
            if first:
                acc[rows, :] = value
            else:
                acc[rows, :] += value
            return carry

        lax.fori_loop(0, 2, rows_step, 0)

    def project_many(lo, hi):
        def step(k, carry):
            project(k, False)
            return carry

        lax.fori_loop(lo, hi, step, 0)

    near_k, far_k = yl * 4, (1 - yl) * 4
    project(near_k, True)
    project_many(near_k + 1, near_k + 3)
    relay("i", gi, "oth", 3, "rest")
    swap_both("i", gi, "oth", 3)
    project_many(near_k + 3, near_k + 4)
    relay("o", go, "own", 4, "lead", False)
    cross("o", go, 4)
    swap("o", go, "own", 4)
    for dz in (0, 1, -1, 2, -2, 3, -3):
        take_swap("i", gi, "oth", dz)
    last = lax.div(lax.rem(z + 4, NZ), 2)

    def far_step(j, carry):
        project(far_k + lax.rem(last + 1 + j, 4), False)
        return carry

    lax.fori_loop(0, 2, far_step, 0)
    relay("i", gi, "oth", 4, "lead", False)
    swap("i", gi, "oth", 4)
    lax.fori_loop(2, 3, far_step, 0)
    take_swap("i", gi, "oth", 4)
    lax.fori_loop(3, 4, far_step, 0)

    def head_norm(v, gain):
        v = v - jnp.mean(v, -1, keepdims=True)
        var = jnp.mean(v * v, -1, keepdims=True)
        return (v * lax.rsqrt(var + EPS) * gain).astype(BF16)

    def attend(i, carry):
        rows = pl.ds(pl.multiple_of(i * PATCHES, PATCHES), PATCHES)
        for h in range(3):
            lo = h * 3 * HEAD_DIM
            q = head_norm(acc[rows, lo:lo + HEAD_DIM], qg_ref[...].reshape(1, HEAD_DIM))
            k = head_norm(acc[rows, lo + HEAD_DIM:lo + 2 * HEAD_DIM], kg_ref[...].reshape(1, HEAD_DIM))
            v = acc[rows, lo + 2 * HEAD_DIM:lo + 3 * HEAD_DIM].astype(BF16)
            s = dot_nt(q, k) / math.sqrt(HEAD_DIM)
            e = jnp.exp(s - jnp.max(s, -1, keepdims=True))
            p = (e / jnp.sum(e, -1, keepdims=True)).astype(BF16)
            o = jnp.dot(p, v, preferred_element_type=F32)
            mixed[rows, h * HEAD_DIM:(h + 1) * HEAD_DIM] = o.astype(BF16)
        return carry

    lax.fori_loop(0, 2, attend, 0)

    for dz in (0, 1, -1, 2, -2, 3, -3, 4):
        take_cross("o", go, dz)
        swap("o", go, "oth", dz)
    for col in ("own", "oth"):
        for dz in (0, 1, -1, 2, -2, 3, -3, 4):
            take_swap("o", go, col, dz)

    def out_part(t):
        w = go[pl.ds(t * 4, 4)].reshape(768, 384)
        part[t] = dot_nt(mixed[...], w).astype(BF16)

    a_rows, b_rows = pl.ds(0, 256), pl.ds(256, 256)
    span = {"+": a_rows, "-": b_rows}
    other = {"+": b_rows, "-": a_rows}
    ys = {"p": 1 - yh, "o": yh}
    near = {"+": xp, "-": xm}

    far_p, far_o = xf * 2 + ys["p"], xf * 2 + ys["o"]
    out_part(far_p)
    push("fh", part.at[far_p], r4, "h")
    for sign in "+-":
        t = near[sign] * 2 + ys["p"]
        out_part(t)
        for i, rows in enumerate((a_rows, b_rows)):
            push("n" + sign + "p" + str(i), part.at[t, rows], r2.at[0, "+-".index(sign), rows], "x" + sign)
    out_part(far_o)
    for sign in "+-":
        out_part(near[sign] * 2 + ys["o"])
    for g in "po":
        out_part(x * 2 + ys[g])

    def squares(ref, r, total):
        v = ref[r].astype(F32)
        v = v * v
        w = v.shape[1]
        row = v[:, :128]
        for j in range(1, w // 128):
            row = row + v[:, j * 128:(j + 1) * 128]
        return total + jnp.sum(row.reshape(24, 8, 128), 0)

    zero = jnp.zeros((8, 128), F32)
    nown[0, pl.ds(0, 8), :] = lax.fori_loop(0, 32, lambda r, t: squares(gi, r, t), zero)
    nown[0, pl.ds(8, 8), :] = lax.fori_loop(0, 32, lambda r, t: squares(go, r, t), zero)

    x1 = x + 1 - 2 * lax.rem(x, 2)
    dev["n0"] = dev["h"]
    dev["n1"] = (rep, x1 * 2 + yh)
    dev["n2"] = (rep, (NX - 1 - x) * 2 + yh)

    def norm_push(s):
        push("norm" + str(s), nown.at[s], nrecv.at[s], "n" + str(s))

    def norm_take(s):
        take("norm" + str(s), nrecv.at[s])
        nown[s + 1] = nown[s] + nrecv[s]

    norm_push(0)

    mine = x * 2 + yh
    theirs = x * 2 + 1 - yh

    def hand_over(n):
        rows = (a_rows, b_rows)[n]
        for i, sign in enumerate("+-"):
            take("n" + sign + "p" + str(n), r2.at[0, i, rows])
        total = part[theirs, rows].astype(F32) + r2[0, 0, rows].astype(F32) + r2[0, 1, rows].astype(F32)
        tsum[rows] = total.astype(BF16)
        push("t" + str(n), tsum.at[rows], r3.at[rows], "h")

    hand_over(0)
    take("fh", r4)
    for i, sign in enumerate("+-"):
        rows = span[sign]
        part[far_o, rows] = (part[far_o, rows].astype(F32) + r4[rows].astype(F32)).astype(BF16)
        push("f" + sign, part.at[far_o, rows], r1.at[i], "x" + sign)
    for i, sign in enumerate("+-"):
        t = near[sign] * 2 + yh
        push("n" + sign + "od", part.at[t, other[sign]], r2.at[1, i, other[sign]], "x" + sign)
    hand_over(1)
    norm_take(0)
    norm_push(1)
    for i, sign in enumerate("+-"):
        t = near[sign] * 2 + yh
        take("f" + sign, r1.at[i])
        part[t, span[sign]] = (part[t, span[sign]].astype(F32) + r1[i].astype(F32)).astype(BF16)
        push("n" + sign + "os", part.at[t, span[sign]], r2.at[1, i, span[sign]], "x" + sign)
    norm_take(1)
    norm_push(2)
    for i, sign in enumerate("+-"):
        take("n" + sign + "od", r2.at[1, i, other[sign]])
    for n, rows in enumerate((a_rows, b_rows)):
        take("t" + str(n), r3.at[rows])
    norm_take(2)
    total_in = jnp.sum(nown[3, pl.ds(0, 8), :], keepdims=True)
    total_out = jnp.sum(nown[3, pl.ds(8, 8), :], keepdims=True)
    norm_ref[0] = (total_in / (3 * HEADS * HEAD_DIM))[0, 0]
    norm_ref[1] = (total_out / D)[0, 0]
    for i, sign in enumerate("+-"):
        take("n" + sign + "os", r2.at[1, i, span[sign]])
    for rows in (a_rows, b_rows):
        total = part[mine, rows].astype(F32) + r2[1, 0, rows].astype(F32) + r2[1, 1, rows].astype(F32)
        out_ref[rows] = (total + r3[rows].astype(F32)).astype(BF16)
    sent("")
    assert len(ids) <= NSEM


def shards(activations, norm_gain, query_gain, key_gain, project_in, project_out):
    rows, cols = activations.shape
    hbm = pl.BlockSpec(memory_space=pl.ANY)
    vmem = pl.BlockSpec(memory_space=pltpu.VMEM)
    out, norms = pl.pallas_call(
        kernel,
        name="block",
        out_shape=(jax.ShapeDtypeStruct((rows, cols), BF16), jax.ShapeDtypeStruct((2,), F32)),
        in_specs=[hbm, vmem, vmem, vmem, hbm, hbm],
        out_specs=(vmem, pl.BlockSpec(memory_space=pltpu.SMEM)),
        scratch_shapes=[
            pltpu.VMEM((32, 192, 1152), BF16),
            pltpu.VMEM((32, 192, 384), BF16),
            pltpu.VMEM((8, 512, 768), BF16),
            pltpu.VMEM((512, 1152), F32),
            pltpu.VMEM((512, 384), BF16),
            pltpu.VMEM((8, 512, 768), BF16),
            pltpu.VMEM((2, 256, 768), BF16),
            pltpu.VMEM((2, 2, 512, 768), BF16),
            pltpu.VMEM((512, 768), BF16),
            pltpu.VMEM((512, 768), BF16),
            pltpu.VMEM((512, 768), BF16),
            pltpu.VMEM((4, 16, 128), F32),
            pltpu.VMEM((3, 16, 128), F32),
            pltpu.SemaphoreType.DMA((NSEM,)),
            pltpu.SemaphoreType.DMA((NSEM,)),
            pltpu.SemaphoreType.DMA((5,)),
        ],
        compiler_params=pltpu.CompilerParams(
            collective_id=0, has_side_effects=True, vmem_limit_bytes=63 * 1024 * 1024
        ),
    )(
        activations,
        norm_gain,
        query_gain,
        key_gain,
        project_in.transpose(1, 0, 2),
        project_out,
    )
    return out, jnp.sqrt(norms)


def solution(mesh):
    return jax.shard_map(
        shards,
        mesh=mesh,
        in_specs=(P("rep", "tp"), P(), P(), P(), P("rep", "tp", None), P("rep", "tp")),
        out_specs=(P("rep", "tp"), P()),
        check_vma=False,
    )
```

time: 184 us -> 143 us (0.78)
  Pallas kernels: 175 us -> 138 us
  local copies, waits for them, and re-layouts: 6.5 us -> 3.19 us
    pallas_call x1, Pallas kernels: 175 us -> 138 us  [shards(): pl.pallas_call(kernel, name='block', out_shape=(jax.ShapeDtypeStruct((row...]
    reshape x2 -> x0, local copies, waits for them, and re-layouts: 3.16 us -> none  [the longest x1 1.82 us: shards(): project_in.reshape(depth, -1)]
where the time goes in v2:
time: 143 us; the launch traced here: 142 us
  Pallas kernels  138 us (97%)
  local copies, waits for them, and re-layouts  3.19 us (2%)
    pallas_call x1, Pallas kernels, shards(): pl.pallas_call(kernel, name='block', out_shape=(jax.ShapeDtypeStruct((row...  138 us

profile of v2, /device:TPU:32, one launch (start us, length us, event | category | flops | bytes accessed | tf_op | source)
XLA Modules:
  0.0 141.9 jit_solution(14594329692032920777)
XLA Ops:
  0.6 138.0 %block.1 = (bf16[512,768]{1,0:T(8,128)(2,1)}, f32[2]{0:T(128)}) custom-call(bf16[512,768]{1,0:T(8,128)(2,1)} %x_ref.1, f32[6144]{0:T(1024)} %gain_ref.1, f32[128]{0:T(128)} %qg_ref.1, f32[128]{0:T(128)} %kg_ref.1, bf16[3,192,384]{2,1,0:T(8,128)(2,1)} %bitcast.1, bf16[192,384]{1,0:T(8,128)(2,1)} %wo_ref.1), custom_call_target="tpu_custom_call" | custom-call | tf_op jit(solution)/shard_map/block/pallas_call | solution.py:429
  138.7 0.0 copy-start
  138.7 0.6 copy-done
  139.3 0.5 sqrt.3
  139.8 2.1 %copy.9 = bf16[512,768]{1,0:T(8,128)(2,1)} copy(bf16[512,768]{1,0:T(8,128)(2,1)} %get-tuple-element.8) | data formatting | bytes 1572864
Async XLA Ops:
  138.7 0.6 copy-start

commit v3 on v2

v3 whole, which is shorter than its diff:
```python
import math

import jax
import jax.numpy as jnp
from jax import lax
from jax.experimental import pallas as pl
from jax.experimental.pallas import tpu as pltpu
from jax.sharding import PartitionSpec as P

D = 6144
HEADS = 24
HEAD_DIM = 128
PATCHES = 256
NX, NZ = 4, 8
MESH = pl.DeviceIdType.MESH
F32, BF16 = jnp.float32, jnp.bfloat16
EPS = 1e-06
NSEM = 85


def dot_nt(a, b):
    return lax.dot_general(a, b, (((1,), (1,)), ((), ())), preferred_element_type=F32)


def kernel(
    x_ref, gain_ref, qg_ref, kg_ref, w_ref, wo_ref, out_ref, norm_ref,
    gi, go, xg, means, spread, stage, acc, mixed, part, r1, r2, r3, r4, tsum, nown, nrecv,
    send, recv, local,
):
    rep, tp = lax.axis_index("rep"), lax.axis_index("tp")
    c = lax.rem(rep, 2)
    z = lax.rem(lax.div(rep, 2), NZ)
    yl = lax.div(rep, 2 * NZ)
    x, yh = lax.div(tp, 2), lax.rem(tp, 2)

    def rep_of(yl_, z_, c_):
        return (yl_ * NZ + z_) * 2 + c_

    zp, zm = lax.rem(z + 1, NZ), lax.rem(z + NZ - 1, NZ)
    xp, xm = lax.rem(x + 1, NX), lax.rem(x + NX - 1, NX)
    xf = lax.rem(x + 2, NX)
    dev = {
        "z+": (rep_of(yl, zp, c), tp),
        "z-": (rep_of(yl, zm, c), tp),
        "c": (rep_of(yl, z, 1 - c), tp),
        "y": (rep_of(1 - yl, z, c), tp),
        "x+": (rep, xp * 2 + yh),
        "x-": (rep, xm * 2 + yh),
        "h": (rep, x * 2 + 1 - yh),
    }

    ids, parity = {}, [None]
    groups = "aiors"
    sizes = {(g, which): 0 for g in groups for which in (None, 0, 1)}

    def on(which, action):
        @pl.when(lax.rem(z, 2) == which)
        def _():
            parity[0] = which
            action()
            parity[0] = None

    def ident(name):
        return ids.setdefault(name, len(ids))

    def push(name, src, dst, to, group=None):
        k = ident(name)
        group = group or name[0]
        pltpu.make_async_remote_copy(
            src_ref=src, dst_ref=dst, send_sem=send.at[groups.index(group)], recv_sem=recv.at[k],
            device_id=dev[to], device_id_type=MESH,
        ).start()
        sizes[group, parity[0]] += math.prod(src.shape)

    def take(name, dst):
        k = ident(name)
        pltpu.make_async_remote_copy(
            src_ref=dst, dst_ref=dst, send_sem=send.at[0], recv_sem=recv.at[k],
            device_id=dev["c"], device_id_type=MESH,
        ).wait_recv()

    def sent(group, which=None):
        like = {"a": xg, "i": gi, "o": go, "r": part, "s": nown}[group]
        total = sizes[group, None] + (sizes[group, which] if which is not None else 0)
        count, rest = divmod(total, math.prod(like.shape[1:]))
        assert rest == 0 and count <= like.shape[0]
        ref = like.at[pl.ds(0, count)]
        pltpu.make_async_remote_copy(
            src_ref=ref, dst_ref=ref, send_sem=send.at[groups.index(group)], recv_sem=recv.at[0],
            device_id=dev["c"], device_id_type=MESH,
        ).wait_send()

    table = {
        (other, dz, partner): rep_of(
            1 - yl if other else yl, lax.rem(z + dz + NZ, NZ), 1 - c if partner else c
        )
        for other in (0, 1) for dz in range(-4, 5) for partner in (0, 1)
    }

    def piece(other, dz, partner=0):
        return table[int(other), dz, partner]

    me_r, me_t = piece(0, 0), tp
    own_x, own_w, own_o = xg.at[me_t], gi.at[me_r], go.at[me_r]
    fetch = [pltpu.make_async_copy(x_ref, own_x, local.at[0])]
    for h in range(3):
        fetch.append(pltpu.make_async_copy(w_ref.at[h], own_w.at[:, pl.ds(h * 384, 384)], local.at[1 + h]))
    fetch.append(pltpu.make_async_copy(wo_ref, own_o, local.at[4]))
    for copy in fetch:
        copy.start()

    barrier = pltpu.get_barrier_semaphore()
    for d in dev.values():
        pl.semaphore_signal(barrier, inc=1, device_id=d, device_id_type=MESH)
    pl.semaphore_wait(barrier, len(dev))

    fetch[0].wait()
    push("ah", own_x, own_x, "h")
    push("ax+own", own_x, own_x, "x+")
    push("ax-own", own_x, own_x, "x-")
    for copy in fetch[1:4]:
        copy.wait()
    rows96 = (pl.ds(0, 96), pl.ds(96, 96))
    for n in (0, 1):
        for sign, m in (("+", n), ("-", 1 - n)):
            ref = gi.at[me_r, rows96[m]]
            push("iz" + sign + "1own" + str(m), ref, ref, "z" + sign)
    push("icown", own_w, own_w, "c")
    fetch[4].wait()

    def rows_of(ref, n):
        rows = ref.shape[0] // 2
        return ref.at[pl.ds(n * rows, rows)]

    def opp(sign):
        return 1 if sign == "+" else -1

    def lead(sign):
        return 0 if sign == "+" else 1

    def take_z(kind, buf, col, sign, d, n):
        ref = rows_of(buf.at[piece(col == "oth", -opp(sign) * d)], n)
        take(kind + "z" + sign + str(d) + col + str(n), ref)

    def push_z(kind, buf, col, sign, d, n):
        ref = rows_of(buf.at[piece(col == "oth", -opp(sign) * (d - 1))], n)
        push(kind + "z" + sign + str(d) + col + str(n), ref, ref, "z" + sign)

    def swap(col, dz):
        ref = gi.at[piece(col == "oth", dz)]
        push("ic" + (col if dz < 4 or col == "own" else "last"), ref, ref, "c")

    def swap_o(wave, col, dz):
        ref = go.at[piece(col == "oth", dz)]
        push("oc" + str(wave), ref, ref, "c")

    def cross_o(wave, dz):
        ref = go.at[piece(0, dz)]
        push("oy" + str(wave), ref, ref, "y")

    def cross_half(buf, dz, n):
        ref = rows_of(buf.at[piece(0, dz)], n)
        push("iy" + str(dz) + "h" + str(n), ref, ref, "y")

    def take_cross_half(buf, dz, n):
        take("iy" + str(dz) + "h" + str(n), rows_of(buf.at[piece(1, dz)], n))

    tile = {
        "own+": xm * 2 + yh, "own-": xp * 2 + yh,
        "par+": xm * 2 + 1 - yh, "par-": xp * 2 + 1 - yh,
        "ownf": xf * 2 + yh, "parf": xf * 2 + 1 - yh,
    }

    def acts_step(who):
        for sign in "+-":
            ref = xg.at[tile[who + sign]]
            take("ax" + sign + who, ref)
            ref = rows_of(ref, lead(sign))
            push("ax" + sign + who + "f", ref, ref, "x" + sign)

    def acts_far(who):
        for sign in "+-":
            take("ax" + sign + who + "f", rows_of(xg.at[tile[who + "f"]], lead(sign)))

    def relay(kind, buf, col, d, which, onward=True):
        for sign in "+-":
            n = lead(sign) if which == "lead" else 1 - lead(sign)
            take_z(kind, buf, col, sign, d, n)
            if onward and (d < 3 or (d == 3 and which == "lead")):
                push_z(kind, buf, col, sign, d + 1, n)

    def swap_both(col, d):
        for sign in "+-":
            swap(col, -opp(sign) * d)

    def o_ref(col, sign, d, at):
        ref = go.at[piece(col == "oth", -opp(sign) * at)]
        return rows_of(ref, lead(sign)) if d == 4 else ref

    def push_o(col, d):
        for sign in "+-":
            ref = o_ref(col, sign, d, d - 1)
            push("oz" + sign + str(d) + col, ref, ref, "z" + sign)

    def take_o(col, d):
        for sign in "+-":
            take("oz" + sign + str(d) + col, o_ref(col, sign, d, d))

    def offsets(d):
        return (d,) if d in (0, 4) else (-d, d)

    def first_wave(d):
        def step():
            if d:
                take_o("own", d)
            if d < 4:
                push_o("own", d + 1)
            for dz in offsets(d):
                cross_o(1, dz)
                swap_o(1, "own", dz)

        on(d % 2, step)

    def first_wave_over():
        take("oy1", go.at[pl.ds(0, 4)])
        for which in (0, 1):
            def step(which=which):
                for d in range(which, 5, 2):
                    for dz in offsets(d):
                        swap_o(1, "oth", dz)

            on(which, step)

    def second_wave_cross():
        on(1, lambda: cross_o(2, 0))

    def second_wave(d, *cols):
        def step():
            for col in cols:
                if d:
                    take_o(col, d)
                elif col == "oth":
                    take("oy2", go.at[piece(1, 0)])
                if d < 4:
                    push_o(col, d + 1)
                for dz in offsets(d):
                    swap_o(2, col, dz)

        on(1 - d % 2, step)

    def lane_tiles(t, rows):
        return [xg[t, rows, j * 128:(j + 1) * 128].astype(F32) for j in range(6)]

    def measure(t, first=False):
        def step(i, carry):
            for part_ in range(4):
                rows = pl.ds(pl.multiple_of(i * 128 + part_ * 32, 32), 32)
                tiles = lane_tiles(t, rows)
                total = tiles[0]
                for v in tiles[1:]:
                    total = total + v
                mean = jnp.sum(total, -1, keepdims=True) * (1.0 / 768)
                square = jnp.zeros((32, 128), F32)
                for v in tiles:
                    v = v - mean
                    square = square + v * v
                means[t, rows, :] = jnp.broadcast_to(mean, (32, 128))
                spread[rows, :] = square if first else spread[rows, :] + square
            return carry

        lax.fori_loop(0, 4, step, 0)

    def norm_rows(i, carry):
        for part_ in range(4):
            rows = pl.ds(pl.multiple_of(i * 128 + part_ * 32, 32), 32)
            mean = means[0, rows, :]
            for t in range(1, 8):
                mean = mean + means[t, rows, :]
            mean = mean * (1.0 / 8)
            apart = jnp.zeros((32, 128), F32)
            for t in range(8):
                v = means[t, rows, :] - mean
                apart = apart + v * v
            variance = (jnp.sum(spread[rows, :], -1, keepdims=True) + 768.0 * apart) * (1.0 / D)
            scale = lax.rsqrt(variance + EPS)
            for t in range(8):
                for j, v in enumerate(lane_tiles(t, rows)):
                    gain = gain_ref[pl.ds(t * 768 + j * 128, 128)].reshape(1, 128)
                    xg[t, rows, j * 128:(j + 1) * 128] = ((v - mean) * scale * gain).astype(BF16)
        return carry

    measure(me_t, True)
    relay("i", gi, "own", 1, "lead")
    relay("i", gi, "own", 1, "rest")
    for dz, n in ((1, 1), (-1, 0), (1, 0), (-1, 1)):
        cross_half(gi, dz, n)
    for dz in (1, -1):
        swap("own", dz)
    push("iy0", own_w, own_w, "y")
    first_wave(0)
    second_wave_cross()
    relay("i", gi, "own", 2, "lead")
    par = xg.at[x * 2 + 1 - yh]
    take("ah", par)
    push("ax+par", par, par, "x+")
    push("ax-par", par, par, "x-")
    acts_step("own")
    relay("i", gi, "own", 2, "rest")
    swap_both("own", 2)
    measure(x * 2 + 1 - yh)
    for sign in "+-":
        measure(tile["own" + sign])
    relay("i", gi, "own", 3, "lead")
    first_wave(1)
    for dz, sign in ((1, "-"), (-1, "+")):
        take_cross_half(gi, dz, lead(sign))
        push_z("i", gi, "oth", sign, 2, lead(sign))
    relay("i", gi, "own", 3, "rest")
    swap_both("own", 3)
    for dz, sign in ((1, "-"), (-1, "+")):
        take_cross_half(gi, dz, 1 - lead(sign))
        push_z("i", gi, "oth", sign, 2, 1 - lead(sign))
        swap("oth", dz)
    relay("i", gi, "own", 4, "lead", False)
    swap("own", 4)
    acts_step("par")
    for sign in "+-":
        measure(tile["par" + sign])
    first_wave(2)
    relay("i", gi, "oth", 2, "lead")
    acts_far("own")
    measure(tile["ownf"])
    take("iy0", gi.at[piece(1, 0)])
    swap("oth", 0)
    relay("i", gi, "oth", 2, "rest")
    swap_both("oth", 2)
    first_wave(3)
    acts_far("par")
    measure(tile["parf"])
    sent("a")
    lax.fori_loop(0, 4, norm_rows, 0)
    relay("i", gi, "oth", 3, "lead")
    take("icown", gi.at[pl.ds(0, 8)])

    def product(k):
        return jnp.dot(xg[k], gi[pl.ds(k * 4, 4)].reshape(768, 1152), preferred_element_type=F32)

    near_k, far_k = yl * 4, (1 - yl) * 4
    acc[...] = product(near_k) + product(near_k + 1)
    relay("i", gi, "oth", 3, "rest")
    swap_both("oth", 3)
    first_wave(4)
    second_wave(0, "own", "oth")
    acc[...] += product(near_k + 2) + product(near_k + 3)
    take("icoth", gi.at[pl.ds(0, 7)])
    last = lax.div(lax.rem(z + 4, NZ), 2)

    def far_chunk(j):
        return product(far_k + lax.rem(last + 1 + j, 4))

    acc[...] += far_chunk(0) + far_chunk(1)
    relay("i", gi, "oth", 4, "lead", False)
    swap("oth", 4)
    first_wave_over()
    acc[...] += far_chunk(2)
    take("iclast", gi.at[piece(1, 4, 1)])
    acc[...] += far_chunk(3)
    second_wave(1, "own")

    def head_norm(v, gain):
        v = v - jnp.mean(v, -1, keepdims=True)
        var = jnp.mean(v * v, -1, keepdims=True)
        return (v * lax.rsqrt(var + EPS) * gain).astype(BF16)

    def attend(i, carry):
        rows = pl.ds(pl.multiple_of(i * PATCHES, PATCHES), PATCHES)
        for h in range(3):
            lo = h * 3 * HEAD_DIM
            q = head_norm(acc[rows, lo:lo + HEAD_DIM], qg_ref[...].reshape(1, HEAD_DIM))
            k = head_norm(acc[rows, lo + HEAD_DIM:lo + 2 * HEAD_DIM], kg_ref[...].reshape(1, HEAD_DIM))
            v = acc[rows, lo + 2 * HEAD_DIM:lo + 3 * HEAD_DIM].astype(BF16)
            s = dot_nt(q, k) / math.sqrt(HEAD_DIM)
            e = jnp.exp(s - jnp.max(s, -1, keepdims=True))
            p = (e / jnp.sum(e, -1, keepdims=True)).astype(BF16)
            o = jnp.dot(p, v, preferred_element_type=F32)
            mixed[rows, h * HEAD_DIM:(h + 1) * HEAD_DIM] = o.astype(BF16)
        return carry

    lax.fori_loop(0, 2, attend, 0)

    second_wave(1, "oth")
    take("oc1", go.at[pl.ds(0, 8)])

    def out_part(t, n):
        w = go[pl.ds(t * 4 + n * 2, 2)].reshape(384, 384)
        part[t, n] = dot_nt(mixed[...], w).astype(BF16)

    a_rows, b_rows = pl.ds(0, 256), pl.ds(256, 256)
    span = {"+": a_rows, "-": b_rows}
    other = {"+": b_rows, "-": a_rows}
    near_o = {"+": xp * 2 + yh, "-": xm * 2 + yh}
    near_p = {"+": xp * 2 + 1 - yh, "-": xm * 2 + 1 - yh}
    far_o, far_p = xf * 2 + yh, xf * 2 + 1 - yh
    mine, theirs = x * 2 + yh, x * 2 + 1 - yh
    signs = tuple(enumerate("+-"))

    def launch(n):
        for i, sign in signs:
            t = near_p[sign]
            out_part(t, n)
            push("n" + sign + "p" + str(n), part.at[t, n], r2.at[0, i, n], "x" + sign, "r")
        out_part(far_p, n)
        push("fh" + str(n), part.at[far_p, n], r4.at[n], "h", "r")
        for i, sign in signs:
            t = near_o[sign]
            out_part(t, n)
            push("n" + sign + "d" + str(n), part.at[t, n, other[sign]], r2.at[1, i, n, other[sign]], "x" + sign, "r")
        out_part(far_o, n)
        out_part(theirs, n)
        out_part(mine, n)

    def plus(a, b):
        return (a.astype(F32) + b.astype(F32)).astype(BF16)

    def far(n):
        take("fh" + str(n), r4.at[n])
        for i, sign in signs:
            rows = span[sign]
            part[far_o, n, rows] = plus(part[far_o, n, rows], r4[n, rows])
            push("f" + sign + str(n), part.at[far_o, n, rows], r1.at[n, i], "x" + sign, "r")

    def near_add(n):
        for i, sign in signs:
            t, rows = near_o[sign], span[sign]
            take("f" + sign + str(n), r1.at[n, i])
            part[t, n, rows] = plus(part[t, n, rows], r1[n, i])

    def near_push(n):
        for i, sign in signs:
            t, rows = near_o[sign], span[sign]
            push("n" + sign + "s" + str(n), part.at[t, n, rows], r2.at[1, i, n, rows], "x" + sign, "r")

    def hand_over(n):
        for i, sign in signs:
            take("n" + sign + "p" + str(n), r2.at[0, i, n])
        total = part[theirs, n].astype(F32) + r2[0, 0, n].astype(F32) + r2[0, 1, n].astype(F32)
        tsum[n] = total.astype(BF16)
        push("t" + str(n), tsum.at[n], r3.at[n], "h", "r")

    done = []

    def finish(n):
        take("t" + str(n), r3.at[n])
        for i, sign in signs:
            take("n" + sign + "d" + str(n), r2.at[1, i, n, other[sign]])
        for i, sign in signs:
            take("n" + sign + "s" + str(n), r2.at[1, i, n, span[sign]])
            rows = span[sign]
            total = part[mine, n, rows].astype(F32) + r2[1, 0, n, rows].astype(F32)
            total = total + r2[1, 1, n, rows].astype(F32)
            stage[n, rows] = (total + r3[n, rows].astype(F32)).astype(BF16)
            copy = pltpu.make_async_copy(
                stage.at[n, rows], out_ref.at[rows, pl.ds(n * 384, 384)], local.at[2 * n + i]
            )
            copy.start()
            done.append(copy)

    def squares(ref, r, total):
        v = ref[r].astype(F32)
        v = v * v
        row = v[:, :128]
        for j in range(1, v.shape[1] // 128):
            row = row + v[:, j * 128:(j + 1) * 128]
        return total + jnp.sum(row.reshape(24, 8, 128), 0)

    zero = jnp.zeros((8, 128), F32)
    x1 = x + 1 - 2 * lax.rem(x, 2)
    dev["n0"] = dev["c"]
    dev["n1"] = (rep, x1 * 2 + yh)
    dev["n2"] = (rep, (NX - 1 - x) * 2 + yh)
    dev["n3"] = dev["h"]

    def norm_push(k):
        push("norm" + str(k), nown.at[k], nrecv.at[k], "n" + str(k), "s")

    def norm_take(k):
        take("norm" + str(k), nrecv.at[k])
        nown[k + 1] = nown[k] + nrecv[k]

    launch(0)
    second_wave(2, "own")
    nown[0, pl.ds(0, 8), :] = lax.fori_loop(0, 16, lambda r, t: squares(gi, 2 * r + c, t), zero)
    second_wave(2, "oth")
    second_wave(3, "own")
    hand_over(0)
    far(0)
    second_wave(3, "oth")
    second_wave(4, "own", "oth")
    take("oc2", go.at[pl.ds(0, 8)])
    launch(1)
    nown[0, pl.ds(8, 8), :] = lax.fori_loop(0, 16, lambda r, t: squares(go, 2 * r + c, t), zero)
    norm_push(0)
    near_add(0)
    norm_take(0)
    norm_push(1)
    hand_over(1)
    far(1)
    near_push(0)
    norm_take(1)
    norm_push(2)
    near_add(1)
    near_push(1)
    norm_take(2)
    norm_push(3)
    finish(0)
    norm_take(3)
    total_in = jnp.sum(nown[4, pl.ds(0, 8), :], keepdims=True)
    total_out = jnp.sum(nown[4, pl.ds(8, 8), :], keepdims=True)
    norm_ref[0] = (total_in / (3 * HEADS * HEAD_DIM))[0, 0]
    norm_ref[1] = (total_out / D)[0, 0]
    finish(1)
    for copy in done:
        copy.wait()
    for group in "irs":
        sent(group)
    for which in (0, 1):
        pl.when(lax.rem(z, 2) == which)(lambda which=which: sent("o", which))
    assert len(ids) == NSEM, len(ids)


def shards(activations, norm_gain, query_gain, key_gain, project_in, project_out):
    rows, cols = activations.shape
    hbm = pl.BlockSpec(memory_space=pl.ANY)
    vmem = pl.BlockSpec(memory_space=pltpu.VMEM)
    out, norms = pl.pallas_call(
        kernel,
        name="block",
        out_shape=(jax.ShapeDtypeStruct((rows, cols), BF16), jax.ShapeDtypeStruct((2,), F32)),
        in_specs=[hbm, vmem, vmem, vmem, hbm, hbm],
        out_specs=(hbm, pl.BlockSpec(memory_space=pltpu.SMEM)),
        scratch_shapes=[
            pltpu.VMEM((32, 192, 1152), BF16),
            pltpu.VMEM((32, 192, 384), BF16),
            pltpu.VMEM((8, 512, 768), BF16),
            pltpu.VMEM((8, 512, 128), F32),
            pltpu.VMEM((512, 128), F32),
            pltpu.VMEM((2, 512, 384), BF16),
            pltpu.VMEM((512, 1152), F32),
            pltpu.VMEM((512, 384), BF16),
            pltpu.VMEM((8, 2, 512, 384), BF16),
            pltpu.VMEM((2, 2, 256, 384), BF16),
            pltpu.VMEM((2, 2, 2, 512, 384), BF16),
            pltpu.VMEM((2, 512, 384), BF16),
            pltpu.VMEM((2, 512, 384), BF16),
            pltpu.VMEM((2, 512, 384), BF16),
            pltpu.VMEM((5, 16, 128), F32),
            pltpu.VMEM((4, 16, 128), F32),
            pltpu.SemaphoreType.DMA((5,)),
            pltpu.SemaphoreType.DMA((NSEM,)),
            pltpu.SemaphoreType.DMA((5,)),
        ],
        compiler_params=pltpu.CompilerParams(
            collective_id=0, has_side_effects=True, vmem_limit_bytes=63 * 1024 * 1024
        ),
    )(
        activations,
        norm_gain,
        query_gain,
        key_gain,
        project_in.transpose(1, 0, 2),
        project_out,
    )
    return out, jnp.sqrt(norms)


def solution(mesh):
    return jax.shard_map(
        shards,
        mesh=mesh,
        in_specs=(P("rep", "tp"), P(), P(), P(), P("rep", "tp", None), P("rep", "tp")),
        out_specs=(P("rep", "tp"), P()),
        check_vma=False,
    )
```

time: 143 us -> 133 us (0.930)
  Pallas kernels: 138 us -> 128 us
    pallas_call x1, Pallas kernels: 138 us -> 128 us  [shards(): pl.pallas_call(kernel, name='block', out_shape=(jax.ShapeDtypeStruct((row...]
where the time goes in v3:
time: 133 us; the launch traced here: 132 us
  Pallas kernels  128 us (96%)
  local copies, waits for them, and re-layouts  3.19 us (2%)
    pallas_call x1, Pallas kernels, shards(): pl.pallas_call(kernel, name='block', out_shape=(jax.ShapeDtypeStruct((row...  128 us
    unnamed x3, local copies, waits for them, and re-layouts  2.67 us

profile of v3, /device:TPU:32, one launch (start us, length us, event | category | flops | bytes accessed | tf_op | source)
XLA Modules:
  0.0 131.8 jit_solution(11540860519170903566)
XLA Ops:
  0.6 127.9 %block.1 = (bf16[512,768]{1,0:T(8,128)(2,1)}, f32[2]{0:T(128)}) custom-call(bf16[512,768]{1,0:T(8,128)(2,1)} %x_ref.1, f32[6144]{0:T(1024)} %gain_ref.1, f32[128]{0:T(128)} %qg_ref.1, f32[128]{0:T(128)} %kg_ref.1, bf16[3,192,384]{2,1,0:T(8,128)(2,1)} %bitcast.1, bf16[192,384]{1,0:T(8,128)(2,1)} %wo_ref.1), custom_call_target="tpu_custom_call" | custom-call | tf_op jit(solution)/shard_map/block/pallas_call | solution.py:535
  128.6 0.0 copy-start
  128.6 0.6 copy-done
  129.2 0.5 sqrt.3
  129.7 2.1 %copy.9 = bf16[512,768]{1,0:T(8,128)(2,1)} copy(bf16[512,768]{1,0:T(8,128)(2,1)} %get-tuple-element.8) | data formatting | bytes 1572864
Async XLA Ops:
  128.6 0.6 copy-start

commit v4 on v3

--- a/solution.py
+++ b/solution.py
@@ -15,7 +15,7 @@
 MESH = pl.DeviceIdType.MESH
 F32, BF16 = jnp.float32, jnp.bfloat16
 EPS = 1e-06
-NSEM = 85
+NSEM = 96
 
 
 def dot_nt(a, b):
@@ -42,6 +42,8 @@
     dev = {
         "z+": (rep_of(yl, zp, c), tp),
         "z-": (rep_of(yl, zm, c), tp),
+        "z++": (rep_of(yl, lax.rem(z + 2, NZ), c), tp),
+        "z--": (rep_of(yl, lax.rem(z + NZ - 2, NZ), c), tp),
         "c": (rep_of(yl, z, 1 - c), tp),
         "y": (rep_of(1 - yl, z, c), tp),
         "x+": (rep, xp * 2 + yh),
@@ -50,7 +52,7 @@
     }
 
     ids, parity = {}, [None]
-    groups = "aiors"
+    groups = "aiorsw"
     sizes = {(g, which): 0 for g in groups for which in (None, 0, 1)}
 
     def on(which, action):
@@ -80,7 +82,7 @@
         ).wait_recv()
 
     def sent(group, which=None):
-        like = {"a": xg, "i": gi, "o": go, "r": part, "s": nown}[group]
+        like = {"a": xg, "i": gi, "o": go, "w": go, "r": part, "s": nown}[group]
         total = sizes[group, None] + (sizes[group, which] if which is not None else 0)
         count, rest = divmod(total, math.prod(like.shape[1:]))
         assert rest == 0 and count <= like.shape[0]
@@ -148,15 +150,15 @@
 
     def swap(col, dz):
         ref = gi.at[piece(col == "oth", dz)]
-        push("ic" + (col if dz < 4 or col == "own" else "last"), ref, ref, "c")
+        push("ic" + (col if abs(dz) < 3 or col == "own" else str(abs(dz))), ref, ref, "c")
 
     def swap_o(wave, col, dz):
         ref = go.at[piece(col == "oth", dz)]
-        push("oc" + str(wave), ref, ref, "c")
+        push("oc" + str(wave), ref, ref, "c", " ow"[wave])
 
     def cross_o(wave, dz):
         ref = go.at[piece(0, dz)]
-        push("oy" + str(wave), ref, ref, "y")
+        push("oy" + str(wave), ref, ref, "y", " ow"[wave])
 
     def cross_half(buf, dz, n):
         ref = rows_of(buf.at[piece(0, dz)], n)
@@ -164,6 +166,10 @@
 
     def take_cross_half(buf, dz, n):
         take("iy" + str(dz) + "h" + str(n), rows_of(buf.at[piece(1, dz)], n))
+
+    def quarter(col, sign, over_y):
+        rows = 96 * (1 - lead(sign)) + (0 if over_y else 48)
+        return gi.at[piece(col == "oth", -opp(sign) * (2 if over_y else 1)), pl.ds(rows, 48)]
 
     tile = {
         "own+": xm * 2 + yh, "own-": xp * 2 + yh,
@@ -234,19 +240,50 @@
     def second_wave_cross():
         on(1, lambda: cross_o(2, 0))
 
-    def second_wave(d, *cols):
+    def push_two(col, d):
+        for step in (2, 1):
+            for sign in "+-":
+                ref = o_ref(col, sign, d + step, d)
+                push("oz" + sign + str(d + step) + col + "w", ref, ref, "z" + sign * step, "w")
+
+    def take_two(col, d):
+        for sign in "+-":
+            take("oz" + sign + str(d) + col + "w", o_ref(col, sign, d, d))
+        for dz in offsets(d):
+            swap_o(2, col, dz)
+
+    def second_wave_start():
         def step():
-            for col in cols:
-                if d:
-                    take_o(col, d)
-                elif col == "oth":
-                    take("oy2", go.at[piece(1, 0)])
-                if d < 4:
-                    push_o(col, d + 1)
-                for dz in offsets(d):
-                    swap_o(2, col, dz)
-
-        on(1 - d % 2, step)
+            push_two("own", 0)
+            swap_o(2, "own", 0)
+            take("oy2", go.at[piece(1, 0)])
+            push_two("oth", 0)
+            swap_o(2, "oth", 0)
+
+        on(1, step)
+
+    def second_wave_relay(col):
+        def step():
+            for sign in "+-":
+                take("oz" + sign + "2" + col + "w", o_ref(col, sign, 2, 2))
+            push_two(col, 2)
+            for dz in offsets(2):
+                swap_o(2, col, dz)
+
+        on(1, step)
+
+    def second_wave_leaf(first):
+        def even():
+            for col in ("own", "oth"):
+                take_two(col, 1 if first else 3)
+
+        def odd():
+            for col in ("own", "oth"):
+                take_two(col, 4)
+
+        on(0, even)
+        if not first:
+            on(1, odd)
 
     def lane_tiles(t, rows):
         return [xg[t, rows, j * 128:(j + 1) * 128].astype(F32) for j in range(6)]
@@ -296,9 +333,7 @@
         cross_half(gi, dz, n)
     for dz in (1, -1):
         swap("own", dz)
-    push("iy0", own_w, own_w, "y")
     first_wave(0)
-    second_wave_cross()
     relay("i", gi, "own", 2, "lead")
     par = xg.at[x * 2 + 1 - yh]
     take("ah", par)
@@ -306,6 +341,11 @@
     push("ax-par", par, par, "x-")
     acts_step("own")
     relay("i", gi, "own", 2, "rest")
+    for sign in "-+":
+        ref = quarter("own", sign, True)
+        push("iyq" + sign, ref, ref, "y")
+    push("iy0", own_w, own_w, "y")
+    second_wave_cross()
     swap_both("own", 2)
     measure(x * 2 + 1 - yh)
     for sign in "+-":
@@ -319,7 +359,8 @@
     swap_both("own", 3)
     for dz, sign in ((1, "-"), (-1, "+")):
         take_cross_half(gi, dz, 1 - lead(sign))
-        push_z("i", gi, "oth", sign, 2, 1 - lead(sign))
+        ref = quarter("oth", sign, False)
+        push("izq" + sign, ref, ref, "z" + sign)
         swap("oth", dz)
     relay("i", gi, "own", 4, "lead", False)
     swap("own", 4)
@@ -330,16 +371,21 @@
     relay("i", gi, "oth", 2, "lead")
     acts_far("own")
     measure(tile["ownf"])
-    take("iy0", gi.at[piece(1, 0)])
-    swap("oth", 0)
-    relay("i", gi, "oth", 2, "rest")
+    for sign in "+-":
+        take("iyq" + sign, quarter("oth", sign, True))
+        rows = 96 * (1 - lead(sign)) + 48
+        take("izq" + sign, gi.at[piece(1, -2 * opp(sign)), pl.ds(rows, 48)])
+        push_z("i", gi, "oth", sign, 3, 1 - lead(sign))
     swap_both("oth", 2)
     first_wave(3)
     acts_far("par")
     measure(tile["parf"])
+    take("iy0", gi.at[piece(1, 0)])
+    swap("oth", 0)
     sent("a")
-    lax.fori_loop(0, 4, norm_rows, 0)
+    lax.fori_loop(0, 2, norm_rows, 0)
     relay("i", gi, "oth", 3, "lead")
+    lax.fori_loop(2, 4, norm_rows, 0)
     take("icown", gi.at[pl.ds(0, 8)])
 
     def product(k):
@@ -350,22 +396,24 @@
     relay("i", gi, "oth", 3, "rest")
     swap_both("oth", 3)
     first_wave(4)
-    second_wave(0, "own", "oth")
+    second_wave_start()
     acc[...] += product(near_k + 2) + product(near_k + 3)
-    take("icoth", gi.at[pl.ds(0, 7)])
+    take("icoth", gi.at[pl.ds(0, 5)])
     last = lax.div(lax.rem(z + 4, NZ), 2)
+    odd = lax.rem(z, 2)
 
     def far_chunk(j):
-        return product(far_k + lax.rem(last + 1 + j, 4))
+        return product(far_k + lax.rem(last + (1 + odd, 2 + odd, 3 - 2 * odd, 4)[j], 4))
 
     acc[...] += far_chunk(0) + far_chunk(1)
     relay("i", gi, "oth", 4, "lead", False)
     swap("oth", 4)
     first_wave_over()
+    take("ic3", gi.at[pl.ds(0, 2)])
     acc[...] += far_chunk(2)
-    take("iclast", gi.at[piece(1, 4, 1)])
+    take("ic4", gi.at[piece(1, 4, 1)])
+    second_wave_relay("own")
     acc[...] += far_chunk(3)
-    second_wave(1, "own")
 
     def head_norm(v, gain):
         v = v - jnp.mean(v, -1, keepdims=True)
@@ -388,7 +436,7 @@
 
     lax.fori_loop(0, 2, attend, 0)
 
-    second_wave(1, "oth")
+    second_wave_relay("oth")
     take("oc1", go.at[pl.ds(0, 8)])
 
     def out_part(t, n):
@@ -411,6 +459,8 @@
             push("n" + sign + "p" + str(n), part.at[t, n], r2.at[0, i, n], "x" + sign, "r")
         out_part(far_p, n)
         push("fh" + str(n), part.at[far_p, n], r4.at[n], "h", "r")
+
+    def launch_rest(n):
         for i, sign in signs:
             t = near_o[sign]
             out_part(t, n)
@@ -488,16 +538,15 @@
         nown[k + 1] = nown[k] + nrecv[k]
 
     launch(0)
-    second_wave(2, "own")
-    nown[0, pl.ds(0, 8), :] = lax.fori_loop(0, 16, lambda r, t: squares(gi, 2 * r + c, t), zero)
-    second_wave(2, "oth")
-    second_wave(3, "own")
+    second_wave_leaf(True)
+    launch_rest(0)
+    second_wave_leaf(False)
     hand_over(0)
     far(0)
-    second_wave(3, "oth")
-    second_wave(4, "own", "oth")
     take("oc2", go.at[pl.ds(0, 8)])
     launch(1)
+    launch_rest(1)
+    nown[0, pl.ds(0, 8), :] = lax.fori_loop(0, 16, lambda r, t: squares(gi, 2 * r + c, t), zero)
     nown[0, pl.ds(8, 8), :] = lax.fori_loop(0, 16, lambda r, t: squares(go, 2 * r + c, t), zero)
     norm_push(0)
     near_add(0)
@@ -524,7 +573,7 @@
     for group in "irs":
         sent(group)
     for which in (0, 1):
-        pl.when(lax.rem(z, 2) == which)(lambda which=which: sent("o", which))
+        pl.when(lax.rem(z, 2) == which)(lambda which=which: (sent("o", which), sent("w", which))[0])
     assert len(ids) == NSEM, len(ids)
 
 
@@ -555,7 +604,7 @@
             pltpu.VMEM((2, 512, 384), BF16),
             pltpu.VMEM((5, 16, 128), F32),
             pltpu.VMEM((4, 16, 128), F32),
-            pltpu.SemaphoreType.DMA((5,)),
+            pltpu.SemaphoreType.DMA((6,)),
             pltpu.SemaphoreType.DMA((NSEM,)),
             pltpu.SemaphoreType.DMA((5,)),
         ],

time: 133 us -> 134 us (level)
    pallas_call x1, Pallas kernels: 128 us -> 129 us  [shards(): pl.pallas_call(kernel, name='block', out_shape=(jax.ShapeDtypeStruct((row...]
where the time goes in v4:
time: 134 us; the launch traced here: 133 us
  Pallas kernels  129 us (96%)
  local copies, waits for them, and re-layouts  3.19 us (2%)
    pallas_call x1, Pallas kernels, shards(): pl.pallas_call(kernel, name='block', out_shape=(jax.ShapeDtypeStruct((row...  129 us

profile of v4, /device:TPU:32, one launch (start us, length us, event | category | flops | bytes accessed | tf_op | source)
XLA Modules:
  0.0 133.2 jit_solution(14406133415317017851)
XLA Ops:
  0.6 129.3 %block.1 = (bf16[512,768]{1,0:T(8,128)(2,1)}, f32[2]{0:T(128)}) custom-call(bf16[512,768]{1,0:T(8,128)(2,1)} %x_ref.1, f32[6144]{0:T(1024)} %gain_ref.1, f32[128]{0:T(128)} %qg_ref.1, f32[128]{0:T(128)} %kg_ref.1, bf16[3,192,384]{2,1,0:T(8,128)(2,1)} %bitcast.1, bf16[192,384]{1,0:T(8,128)(2,1)} %wo_ref.1), custom_call_target="tpu_custom_call" | custom-call | tf_op jit(solution)/shard_map/block/pallas_call | solution.py:584
  130.0 0.0 copy-start
  130.0 0.6 copy-done
  130.6 0.5 sqrt.3
  131.1 2.1 %copy.9 = bf16[512,768]{1,0:T(8,128)(2,1)} copy(bf16[512,768]{1,0:T(8,128)(2,1)} %get-tuple-element.8) | data formatting | bytes 1572864
Async XLA Ops:
  130.0 0.6 copy-start

commit v5 on v4

--- a/solution.py
+++ b/solution.py
@@ -15,7 +15,7 @@
 MESH = pl.DeviceIdType.MESH
 F32, BF16 = jnp.float32, jnp.bfloat16
 EPS = 1e-06
-NSEM = 96
+NSEM = 115
 
 
 def dot_nt(a, b):
@@ -52,7 +52,7 @@
     }
 
     ids, parity = {}, [None]
-    groups = "aiorsw"
+    groups = "abiorsw"
     sizes = {(g, which): 0 for g in groups for which in (None, 0, 1)}
 
     def on(which, action):
@@ -82,7 +82,15 @@
         ).wait_recv()
 
     def sent(group, which=None):
-        like = {"a": xg, "i": gi, "o": go, "w": go, "r": part, "s": nown}[group]
+        if group in "ab":
+            assert sizes[group, None] == 7 * 256 * 768
+            ref = xg.at[pl.ds(0, 7), pl.ds(0, 256)]
+            pltpu.make_async_remote_copy(
+                src_ref=ref, dst_ref=ref, send_sem=send.at[groups.index(group)], recv_sem=recv.at[0],
+                device_id=dev["c"], device_id_type=MESH,
+            ).wait_send()
+            return
+        like = {"i": gi, "o": go, "w": go, "r": part, "s": nown}[group]
         total = sizes[group, None] + (sizes[group, which] if which is not None else 0)
         count, rest = divmod(total, math.prod(like.shape[1:]))
         assert rest == 0 and count <= like.shape[0]
@@ -117,9 +125,14 @@
     pl.semaphore_wait(barrier, len(dev))
 
     fetch[0].wait()
-    push("ah", own_x, own_x, "h")
-    push("ax+own", own_x, own_x, "x+")
-    push("ax-own", own_x, own_x, "x-")
+    def image(ref, i):
+        return ref.at[pl.ds(i * PATCHES, PATCHES)]
+
+    for i in (0, 1):
+        ref = image(own_x, i)
+        push("ah" + str(i), ref, ref, "h", "ab"[i])
+        for sign in "+-":
+            push("ax" + sign + "own" + str(i), ref, ref, "x" + sign, "ab"[i])
     for copy in fetch[1:4]:
         copy.wait()
     rows96 = (pl.ds(0, 96), pl.ds(96, 96))
@@ -177,16 +190,25 @@
         "ownf": xf * 2 + yh, "parf": xf * 2 + 1 - yh,
     }
 
-    def acts_step(who):
-        for sign in "+-":
-            ref = xg.at[tile[who + sign]]
-            take("ax" + sign + who, ref)
-            ref = rows_of(ref, lead(sign))
-            push("ax" + sign + who + "f", ref, ref, "x" + sign)
-
-    def acts_far(who):
-        for sign in "+-":
-            take("ax" + sign + who + "f", rows_of(xg.at[tile[who + "f"]], lead(sign)))
+    def acts_half(t, i, sign):
+        return xg.at[t, pl.ds(i * PATCHES + lead(sign) * 128, 128)]
+
+    def acts_par(i):
+        ref = image(xg.at[x * 2 + 1 - yh], i)
+        take("ah" + str(i), ref)
+        for sign in "+-":
+            push("ax" + sign + "par" + str(i), ref, ref, "x" + sign, "ab"[i])
+
+    def acts_step(who, i):
+        for sign in "+-":
+            t = tile[who + sign]
+            take("ax" + sign + who + str(i), image(xg.at[t], i))
+            ref = acts_half(t, i, sign)
+            push("ax" + sign + who + "f" + str(i), ref, ref, "x" + sign, "ab"[i])
+
+    def acts_far(who, i):
+        for sign in "+-":
+            take("ax" + sign + who + "f" + str(i), acts_half(tile[who + "f"], i, sign))
 
     def relay(kind, buf, col, d, which, onward=True):
         for sign in "+-":
@@ -272,23 +294,23 @@
 
         on(1, step)
 
-    def second_wave_leaf(first):
+    def second_wave_leaf():
         def even():
-            for col in ("own", "oth"):
-                take_two(col, 1 if first else 3)
+            for d in (1, 3):
+                for col in ("own", "oth"):
+                    take_two(col, d)
 
         def odd():
             for col in ("own", "oth"):
                 take_two(col, 4)
 
         on(0, even)
-        if not first:
-            on(1, odd)
+        on(1, odd)
 
     def lane_tiles(t, rows):
         return [xg[t, rows, j * 128:(j + 1) * 128].astype(F32) for j in range(6)]
 
-    def measure(t, first=False):
+    def measure(t, image_, first=False):
         def step(i, carry):
             for part_ in range(4):
                 rows = pl.ds(pl.multiple_of(i * 128 + part_ * 32, 32), 32)
@@ -305,7 +327,7 @@
                 spread[rows, :] = square if first else spread[rows, :] + square
             return carry
 
-        lax.fori_loop(0, 4, step, 0)
+        lax.fori_loop(2 * image_, 2 * image_ + 2, step, 0)
 
     def norm_rows(i, carry):
         for part_ in range(4):
@@ -326,7 +348,25 @@
                     xg[t, rows, j * 128:(j + 1) * 128] = ((v - mean) * scale * gain).astype(BF16)
         return carry
 
-    measure(me_t, True)
+    near_k, far_k = yl * 4, (1 - yl) * 4
+    last = lax.div(lax.rem(z + 4, NZ), 2)
+    odd = lax.rem(z, 2)
+
+    def near_chunks(i, j):
+        rows = pl.ds(i * PATCHES, PATCHES)
+        total = None
+        for k in (near_k + j, near_k + j + 1):
+            w = gi[pl.ds(k * 4, 4)].reshape(768, 1152)
+            value = jnp.dot(xg[k, rows], w, preferred_element_type=F32)
+            total = value if total is None else total + value
+        acc[rows] = total if j == 0 else acc[rows] + total
+
+    def far_chunk(j, rows=slice(None)):
+        k = far_k + lax.rem(last + (1 + odd, 2 + odd, 3 - 2 * odd, 4)[j], 4)
+        return jnp.dot(xg[k, rows], gi[pl.ds(k * 4, 4)].reshape(768, 1152), preferred_element_type=F32)
+
+    for i in (0, 1):
+        measure(me_t, i, True)
     relay("i", gi, "own", 1, "lead")
     relay("i", gi, "own", 1, "rest")
     for dz, n in ((1, 1), (-1, 0), (1, 0), (-1, 1)):
@@ -334,12 +374,9 @@
     for dz in (1, -1):
         swap("own", dz)
     first_wave(0)
+    acts_par(0)
+    acts_step("own", 0)
     relay("i", gi, "own", 2, "lead")
-    par = xg.at[x * 2 + 1 - yh]
-    take("ah", par)
-    push("ax+par", par, par, "x+")
-    push("ax-par", par, par, "x-")
-    acts_step("own")
     relay("i", gi, "own", 2, "rest")
     for sign in "-+":
         ref = quarter("own", sign, True)
@@ -347,16 +384,25 @@
     push("iy0", own_w, own_w, "y")
     second_wave_cross()
     swap_both("own", 2)
-    measure(x * 2 + 1 - yh)
+    measure(x * 2 + 1 - yh, 0)
     for sign in "+-":
-        measure(tile["own" + sign])
+        measure(tile["own" + sign], 0)
     relay("i", gi, "own", 3, "lead")
     first_wave(1)
+    acts_step("par", 0)
+    acts_par(1)
+    acts_step("own", 1)
     for dz, sign in ((1, "-"), (-1, "+")):
         take_cross_half(gi, dz, lead(sign))
         push_z("i", gi, "oth", sign, 2, lead(sign))
+    for sign in "+-":
+        measure(tile["par" + sign], 0)
     relay("i", gi, "own", 3, "rest")
     swap_both("own", 3)
+    acts_far("own", 0)
+    measure(tile["ownf"], 0)
+    acts_far("par", 0)
+    measure(tile["parf"], 0)
     for dz, sign in ((1, "-"), (-1, "+")):
         take_cross_half(gi, dz, 1 - lead(sign))
         ref = quarter("oth", sign, False)
@@ -364,64 +410,59 @@
         swap("oth", dz)
     relay("i", gi, "own", 4, "lead", False)
     swap("own", 4)
-    acts_step("par")
-    for sign in "+-":
-        measure(tile["par" + sign])
+    sent("a")
+    lax.fori_loop(0, 2, norm_rows, 0)
     first_wave(2)
+    take("icown", gi.at[pl.ds(0, 8)])
+    near_chunks(0, 0)
     relay("i", gi, "oth", 2, "lead")
-    acts_far("own")
-    measure(tile["ownf"])
+    acts_step("par", 1)
+    near_chunks(0, 2)
     for sign in "+-":
         take("iyq" + sign, quarter("oth", sign, True))
         rows = 96 * (1 - lead(sign)) + 48
         take("izq" + sign, gi.at[piece(1, -2 * opp(sign)), pl.ds(rows, 48)])
         push_z("i", gi, "oth", sign, 3, 1 - lead(sign))
     swap_both("oth", 2)
+    measure(x * 2 + 1 - yh, 1)
+    for who in ("own", "par"):
+        for sign in "+-":
+            measure(tile[who + sign], 1)
+    acts_far("own", 1)
+    measure(tile["ownf"], 1)
     first_wave(3)
-    acts_far("par")
-    measure(tile["parf"])
+    acts_far("par", 1)
+    measure(tile["parf"], 1)
     take("iy0", gi.at[piece(1, 0)])
     swap("oth", 0)
-    sent("a")
-    lax.fori_loop(0, 2, norm_rows, 0)
+    sent("b")
+    lax.fori_loop(2, 3, norm_rows, 0)
     relay("i", gi, "oth", 3, "lead")
-    lax.fori_loop(2, 4, norm_rows, 0)
-    take("icown", gi.at[pl.ds(0, 8)])
-
-    def product(k):
-        return jnp.dot(xg[k], gi[pl.ds(k * 4, 4)].reshape(768, 1152), preferred_element_type=F32)
-
-    near_k, far_k = yl * 4, (1 - yl) * 4
-    acc[...] = product(near_k) + product(near_k + 1)
+    lax.fori_loop(3, 4, norm_rows, 0)
+    near_chunks(1, 0)
     relay("i", gi, "oth", 3, "rest")
     swap_both("oth", 3)
     first_wave(4)
+    near_chunks(1, 2)
     second_wave_start()
-    acc[...] += product(near_k + 2) + product(near_k + 3)
     take("icoth", gi.at[pl.ds(0, 5)])
-    last = lax.div(lax.rem(z + 4, NZ), 2)
-    odd = lax.rem(z, 2)
-
-    def far_chunk(j):
-        return product(far_k + lax.rem(last + (1 + odd, 2 + odd, 3 - 2 * odd, 4)[j], 4))
-
     acc[...] += far_chunk(0) + far_chunk(1)
+    take("ic3", gi.at[pl.ds(0, 2)])
     relay("i", gi, "oth", 4, "lead", False)
     swap("oth", 4)
+    acc[...] += far_chunk(2)
     first_wave_over()
-    take("ic3", gi.at[pl.ds(0, 2)])
-    acc[...] += far_chunk(2)
+    second_wave_relay("own")
     take("ic4", gi.at[piece(1, 4, 1)])
-    second_wave_relay("own")
-    acc[...] += far_chunk(3)
 
     def head_norm(v, gain):
         v = v - jnp.mean(v, -1, keepdims=True)
         var = jnp.mean(v * v, -1, keepdims=True)
         return (v * lax.rsqrt(var + EPS) * gain).astype(BF16)
 
-    def attend(i, carry):
-        rows = pl.ds(pl.multiple_of(i * PATCHES, PATCHES), PATCHES)
+    def attend(i):
+        rows = pl.ds(i * PATCHES, PATCHES)
+        acc[rows] += far_chunk(3, rows)
         for h in range(3):
             lo = h * 3 * HEAD_DIM
             q = head_norm(acc[rows, lo:lo + HEAD_DIM], qg_ref[...].reshape(1, HEAD_DIM))
@@ -432,12 +473,7 @@
             p = (e / jnp.sum(e, -1, keepdims=True)).astype(BF16)
             o = jnp.dot(p, v, preferred_element_type=F32)
             mixed[rows, h * HEAD_DIM:(h + 1) * HEAD_DIM] = o.astype(BF16)
-        return carry
-
-    lax.fori_loop(0, 2, attend, 0)
-
-    second_wave_relay("oth")
-    take("oc1", go.at[pl.ds(0, 8)])
+
 
     def out_part(t, n):
         w = go[pl.ds(t * 4 + n * 2, 2)].reshape(384, 384)
@@ -452,19 +488,31 @@
     mine, theirs = x * 2 + yh, x * 2 + 1 - yh
     signs = tuple(enumerate("+-"))
 
-    def launch(n):
+    def launch_near(n, i):
+        rows = pl.ds(i * PATCHES, PATCHES)
+        w_of = lambda t: go[pl.ds(t * 4 + n * 2, 2)].reshape(384, 384)
+        for k, sign in signs:
+            t = near_p[sign]
+            part[t, n, rows] = dot_nt(mixed[rows], w_of(t)).astype(BF16)
+            ref = part.at[t, n, rows]
+            push("n" + sign + "p" + str(n) + str(i), ref, r2.at[0, k, n, rows], "x" + sign, "r")
+
+    def launch_far(n, i):
+        rows = pl.ds(i * PATCHES, PATCHES)
+        w = go[pl.ds(far_p * 4 + n * 2, 2)].reshape(384, 384)
+        part[far_p, n, rows] = dot_nt(mixed[rows], w).astype(BF16)
+        push("fh" + str(n) + str(i), part.at[far_p, n, rows], r4.at[n, rows], "h", "r")
+
+    def direct(n, j):
         for i, sign in signs:
-            t = near_p[sign]
-            out_part(t, n)
-            push("n" + sign + "p" + str(n), part.at[t, n], r2.at[0, i, n], "x" + sign, "r")
-        out_part(far_p, n)
-        push("fh" + str(n), part.at[far_p, n], r4.at[n], "h", "r")
+            rows = pl.ds((256 if sign == "+" else 0) + 128 * j, 128)
+            ref = part.at[near_o[sign], n, rows]
+            push("n" + sign + "d" + str(n) + str(j), ref, r2.at[1, i, n, rows], "x" + sign, "r")
 
     def launch_rest(n):
         for i, sign in signs:
-            t = near_o[sign]
-            out_part(t, n)
-            push("n" + sign + "d" + str(n), part.at[t, n, other[sign]], r2.at[1, i, n, other[sign]], "x" + sign, "r")
+            out_part(near_o[sign], n)
+        direct(n, 0)
         out_part(far_o, n)
         out_part(theirs, n)
         out_part(mine, n)
@@ -473,9 +521,9 @@
         return (a.astype(F32) + b.astype(F32)).astype(BF16)
 
     def far(n):
-        take("fh" + str(n), r4.at[n])
         for i, sign in signs:
             rows = span[sign]
+            take("fh" + str(n) + str(i), r4.at[n, rows])
             part[far_o, n, rows] = plus(part[far_o, n, rows], r4[n, rows])
             push("f" + sign + str(n), part.at[far_o, n, rows], r1.at[n, i], "x" + sign, "r")
 
@@ -491,8 +539,9 @@
             push("n" + sign + "s" + str(n), part.at[t, n, rows], r2.at[1, i, n, rows], "x" + sign, "r")
 
     def hand_over(n):
-        for i, sign in signs:
-            take("n" + sign + "p" + str(n), r2.at[0, i, n])
+        for j in (0, 1):
+            for i, sign in signs:
+                take("n" + sign + "p" + str(n) + str(j), r2.at[0, i, n, pl.ds(j * PATCHES, PATCHES)])
         total = part[theirs, n].astype(F32) + r2[0, 0, n].astype(F32) + r2[0, 1, n].astype(F32)
         tsum[n] = total.astype(BF16)
         push("t" + str(n), tsum.at[n], r3.at[n], "h", "r")
@@ -502,7 +551,9 @@
     def finish(n):
         take("t" + str(n), r3.at[n])
         for i, sign in signs:
-            take("n" + sign + "d" + str(n), r2.at[1, i, n, other[sign]])
+            for j in (0, 1):
+                rows = pl.ds((256 if sign == "+" else 0) + 128 * j, 128)
+                take("n" + sign + "d" + str(n) + str(j), r2.at[1, i, n, rows])
         for i, sign in signs:
             take("n" + sign + "s" + str(n), r2.at[1, i, n, span[sign]])
             rows = span[sign]
@@ -537,24 +588,34 @@
         take("norm" + str(k), nrecv.at[k])
         nown[k + 1] = nown[k] + nrecv[k]
 
-    launch(0)
-    second_wave_leaf(True)
+    attend(0)
+    take("oc1", go.at[pl.ds(0, 8)])
+    launch_near(0, 0)
+    launch_far(0, 0)
+    attend(1)
+    launch_near(0, 1)
+    launch_far(0, 1)
+    second_wave_relay("oth")
     launch_rest(0)
-    second_wave_leaf(False)
+    nown[0, pl.ds(0, 8), :] = lax.fori_loop(0, 16, lambda r, t: squares(gi, 2 * r + c, t), zero)
     hand_over(0)
     far(0)
+    direct(0, 1)
+    second_wave_leaf()
+    near_add(0)
+    near_push(0)
     take("oc2", go.at[pl.ds(0, 8)])
-    launch(1)
+    for i in (0, 1):
+        launch_near(1, i)
+        launch_far(1, i)
     launch_rest(1)
-    nown[0, pl.ds(0, 8), :] = lax.fori_loop(0, 16, lambda r, t: squares(gi, 2 * r + c, t), zero)
     nown[0, pl.ds(8, 8), :] = lax.fori_loop(0, 16, lambda r, t: squares(go, 2 * r + c, t), zero)
     norm_push(0)
-    near_add(0)
     norm_take(0)
     norm_push(1)
     hand_over(1)
     far(1)
-    near_push(0)
+    direct(1, 1)
     norm_take(1)
     norm_push(2)
     near_add(1)
@@ -604,7 +665,7 @@
             pltpu.VMEM((2, 512, 384), BF16),
             pltpu.VMEM((5, 16, 128), F32),
             pltpu.VMEM((4, 16, 128), F32),
-            pltpu.SemaphoreType.DMA((6,)),
+            pltpu.SemaphoreType.DMA((7,)),
             pltpu.SemaphoreType.DMA((NSEM,)),
             pltpu.SemaphoreType.DMA((5,)),
         ],

time: 134 us -> 131 us (0.978)
  Pallas kernels: 129 us -> 127 us
    pallas_call x1, Pallas kernels: 129 us -> 127 us  [shards(): pl.pallas_call(kernel, name='block', out_shape=(jax.ShapeDtypeStruct((row...]
where the time goes in v5:
time: 131 us
  Pallas kernels  127 us (97%)
  local copies, waits for them, and re-layouts  3.19 us (2%)
    pallas_call x1, Pallas kernels, shards(): pl.pallas_call(kernel, name='block', out_shape=(jax.ShapeDtypeStruct((row...  127 us
    unnamed x3, local copies, waits for them, and re-layouts  2.67 us

profile of v5, /device:TPU:32, one launch (start us, length us, event | category | flops | bytes accessed | tf_op | source)
XLA Modules:
  0.0 131.0 jit_solution(13406127823671733972)
XLA Ops:
  0.6 127.2 %block.1 = (bf16[512,768]{1,0:T(8,128)(2,1)}, f32[2]{0:T(128)}) custom-call(bf16[512,768]{1,0:T(8,128)(2,1)} %x_ref.1, f32[6144]{0:T(1024)} %gain_ref.1, f32[128]{0:T(128)} %qg_ref.1, f32[128]{0:T(128)} %kg_ref.1, bf16[3,192,384]{2,1,0:T(8,128)(2,1)} %bitcast.1, bf16[192,384]{1,0:T(8,128)(2,1)} %wo_ref.1), custom_call_target="tpu_custom_call" | custom-call | tf_op jit(solution)/shard_map/block/pallas_call | solution.py:645
  127.8 0.0 copy-start
  127.9 0.6 copy-done
  128.5 0.5 sqrt.3
  129.0 2.1 %copy.9 = bf16[512,768]{1,0:T(8,128)(2,1)} copy(bf16[512,768]{1,0:T(8,128)(2,1)} %get-tuple-element.8) | data formatting | bytes 1572864
Async XLA Ops:
  127.8 0.6 copy-start

commit v6 on v5

--- a/solution.py
+++ b/solution.py
@@ -181,8 +181,8 @@
         take("iy" + str(dz) + "h" + str(n), rows_of(buf.at[piece(1, dz)], n))
 
     def quarter(col, sign, over_y):
-        rows = 96 * (1 - lead(sign)) + (0 if over_y else 48)
-        return gi.at[piece(col == "oth", -opp(sign) * (2 if over_y else 1)), pl.ds(rows, 48)]
+        rows = 96 * (1 - lead(sign)) + (0 if over_y else 32)
+        return gi.at[piece(col == "oth", -opp(sign) * (2 if over_y else 1)), pl.ds(rows, 32 if over_y else 64)]
 
     tile = {
         "own+": xm * 2 + yh, "own-": xp * 2 + yh,
@@ -420,8 +420,8 @@
     near_chunks(0, 2)
     for sign in "+-":
         take("iyq" + sign, quarter("oth", sign, True))
-        rows = 96 * (1 - lead(sign)) + 48
-        take("izq" + sign, gi.at[piece(1, -2 * opp(sign)), pl.ds(rows, 48)])
+        rows = 96 * (1 - lead(sign)) + 32
+        take("izq" + sign, gi.at[piece(1, -2 * opp(sign)), pl.ds(rows, 64)])
         push_z("i", gi, "oth", sign, 3, 1 - lead(sign))
     swap_both("oth", 2)
     measure(x * 2 + 1 - yh, 1)
@@ -452,7 +452,6 @@
     swap("oth", 4)
     acc[...] += far_chunk(2)
     first_wave_over()
-    second_wave_relay("own")
     take("ic4", gi.at[piece(1, 4, 1)])
 
     def head_norm(v, gain):
@@ -592,15 +591,16 @@
     take("oc1", go.at[pl.ds(0, 8)])
     launch_near(0, 0)
     launch_far(0, 0)
+    second_wave_relay("own")
     attend(1)
     launch_near(0, 1)
     launch_far(0, 1)
     second_wave_relay("oth")
     launch_rest(0)
     nown[0, pl.ds(0, 8), :] = lax.fori_loop(0, 16, lambda r, t: squares(gi, 2 * r + c, t), zero)
-    hand_over(0)
     far(0)
     direct(0, 1)
+    hand_over(0)
     second_wave_leaf()
     near_add(0)
     near_push(0)
@@ -626,8 +626,8 @@
     norm_take(3)
     total_in = jnp.sum(nown[4, pl.ds(0, 8), :], keepdims=True)
     total_out = jnp.sum(nown[4, pl.ds(8, 8), :], keepdims=True)
-    norm_ref[0] = (total_in / (3 * HEADS * HEAD_DIM))[0, 0]
-    norm_ref[1] = (total_out / D)[0, 0]
+    norm_ref[0] = jnp.sqrt(total_in / (3 * HEADS * HEAD_DIM))[0, 0]
+    norm_ref[1] = jnp.sqrt(total_out / D)[0, 0]
     finish(1)
     for copy in done:
         copy.wait()
@@ -636,6 +636,25 @@
     for which in (0, 1):
         pl.when(lax.rem(z, 2) == which)(lambda which=which: (sent("o", which), sent("w", which))[0])
     assert len(ids) == NSEM, len(ids)
+
+
+def deliver(out_ref, norm_ref, to_ref, norms_ref, held, sems, norm_sem):
+    norms = pltpu.make_async_copy(norm_ref, norms_ref, norm_sem)
+    norms.start()
+    parts = held.shape[0]
+    rows = held.shape[1]
+    into, away = [], []
+    for i in range(parts):
+        span = pl.ds(i * rows, rows)
+        into.append(pltpu.make_async_copy(out_ref.at[span], held.at[i], sems.at[0, i]))
+        away.append(pltpu.make_async_copy(held.at[i], to_ref.at[span], sems.at[1, i]))
+        into[-1].start()
+    for i in range(parts):
+        into[i].wait()
+        away[i].start()
+    for copy in away:
+        copy.wait()
+    norms.wait()
 
 
 def shards(activations, norm_gain, query_gain, key_gain, project_in, project_out):
@@ -680,7 +699,15 @@
         project_in.transpose(1, 0, 2),
         project_out,
     )
-    return out, jnp.sqrt(norms)
+    return pl.pallas_call(
+        deliver,
+        name="deliver",
+        out_shape=(jax.ShapeDtypeStruct((rows, cols), BF16), jax.ShapeDtypeStruct((2,), F32)),
+        in_specs=(hbm, hbm),
+        out_specs=(hbm, hbm),
+        scratch_shapes=[pltpu.VMEM((4, rows // 4, cols), BF16), pltpu.SemaphoreType.DMA((2, 4)), pltpu.SemaphoreType.DMA],
+        compiler_params=pltpu.CompilerParams(vmem_limit_bytes=63 * 1024 * 1024),
+    )(out, norms)
 
 
 def solution(mesh):

time: 131 us -> 129 us (0.985)
  local copies, waits for them, and re-layouts: 3.19 us -> 0 us
    unnamed x3 -> x0, local copies, waits for them, and re-layouts: 2.67 us -> none
    pallas_call x0 -> x1, Pallas kernels: none -> 1.98 us  [shards(): pl.pallas_call(deliver, name='deliver', out_shape=(jax.ShapeDtypeStruct((...]
    pallas_call x1, Pallas kernels: 127 us -> 126 us  [shards(): pl.pallas_call(kernel, name='block', out_shape=(jax.ShapeDtypeStruct((row...]
where the time goes in v6:
time: 129 us
  Pallas kernels  128 us (99%)
    pallas_call x1, Pallas kernels, shards(): pl.pallas_call(kernel, name='block', out_shape=(jax.ShapeDtypeStruct((row...  126 us

profile of v6, /device:TPU:32, one launch (start us, length us, event | category | flops | bytes accessed | tf_op | source)
XLA Modules:
  0.0 128.6 jit_solution(2937091915028578657)
XLA Ops:
  0.6 125.8 %block.1 = (bf16[512,768]{1,0:T(8,128)(2,1)}, f32[2]{0:T(128)}) custom-call(bf16[512,768]{1,0:T(8,128)(2,1)} %x_ref.1, f32[6144]{0:T(1024)} %gain_ref.1, f32[128]{0:T(128)} %qg_ref.1, f32[128]{0:T(128)} %kg_ref.1, bf16[3,192,384]{2,1,0:T(8,128)(2,1)} %bitcast.1, bf16[192,384]{1,0:T(8,128)(2,1)} %wo_ref.1), custom_call_target="tpu_custom_call" | custom-call | tf_op jit(solution)/shard_map/block/pallas_call | solution.py:664
  126.5 2.0 %deliver.1 = (bf16[512,768]{1,0:T(8,128)(2,1)}, f32[2]{0:T(128)}) custom-call(bf16[512,768]{1,0:T(8,128)(2,1)} %get-tuple-element.4.out_ref, f32[2]{0:T(128)} %get-tuple-element.5.norm_ref), custom_call_target="tpu_custom_call" | custom-call | tf_op jit(solution)/shard_map/deliver/pallas_call | solution.py:702

commit v7 on v6

--- a/solution.py
+++ b/solution.py
@@ -600,22 +600,22 @@
     nown[0, pl.ds(0, 8), :] = lax.fori_loop(0, 16, lambda r, t: squares(gi, 2 * r + c, t), zero)
     far(0)
     direct(0, 1)
-    hand_over(0)
     second_wave_leaf()
-    near_add(0)
-    near_push(0)
     take("oc2", go.at[pl.ds(0, 8)])
     for i in (0, 1):
         launch_near(1, i)
         launch_far(1, i)
+    hand_over(0)
+    near_add(0)
+    near_push(0)
     launch_rest(1)
     nown[0, pl.ds(8, 8), :] = lax.fori_loop(0, 16, lambda r, t: squares(go, 2 * r + c, t), zero)
     norm_push(0)
+    far(1)
+    direct(1, 1)
     norm_take(0)
     norm_push(1)
     hand_over(1)
-    far(1)
-    direct(1, 1)
     norm_take(1)
     norm_push(2)
     near_add(1)
@@ -623,12 +623,12 @@
     norm_take(2)
     norm_push(3)
     finish(0)
+    finish(1)
     norm_take(3)
     total_in = jnp.sum(nown[4, pl.ds(0, 8), :], keepdims=True)
     total_out = jnp.sum(nown[4, pl.ds(8, 8), :], keepdims=True)
     norm_ref[0] = jnp.sqrt(total_in / (3 * HEADS * HEAD_DIM))[0, 0]
     norm_ref[1] = jnp.sqrt(total_out / D)[0, 0]
-    finish(1)
     for copy in done:
         copy.wait()
     for group in "irs":

time: 129 us -> 131 us (1.016); the launches traced: 129 us -> 129 us
  no operation moved by 1% of the time
where the time goes in v7:
time: 131 us; the launch traced here: 129 us
  Pallas kernels  128 us (98%)
    pallas_call x1, Pallas kernels, shards(): pl.pallas_call(kernel, name='block', out_shape=(jax.ShapeDtypeStruct((row...  126 us

profile of v7, /device:TPU:32, one launch (start us, length us, event | category | flops | bytes accessed | tf_op | source)
XLA Modules:
  0.0 129.2 jit_solution(10218233948094438343)
XLA Ops:
  0.6 126.4 %block.1 = (bf16[512,768]{1,0:T(8,128)(2,1)}, f32[2]{0:T(128)}) custom-call(bf16[512,768]{1,0:T(8,128)(2,1)} %x_ref.1, f32[6144]{0:T(1024)} %gain_ref.1, f32[128]{0:T(128)} %qg_ref.1, f32[128]{0:T(128)} %kg_ref.1, bf16[3,192,384]{2,1,0:T(8,128)(2,1)} %bitcast.1, bf16[192,384]{1,0:T(8,128)(2,1)} %wo_ref.1), custom_call_target="tpu_custom_call" | custom-call | tf_op jit(solution)/shard_map/block/pallas_call | solution.py:664
  127.0 2.0 %deliver.1 = (bf16[512,768]{1,0:T(8,128)(2,1)}, f32[2]{0:T(128)}) custom-call(bf16[512,768]{1,0:T(8,128)(2,1)} %get-tuple-element.4.out_ref, f32[2]{0:T(128)} %get-tuple-element.5.norm_ref), custom_call_target="tpu_custom_call" | custom-call | tf_op jit(solution)/shard_map/deliver/pallas_call | solution.py:702

commit v8 on v7

--- a/solution.py
+++ b/solution.py
@@ -611,10 +611,10 @@
     launch_rest(1)
     nown[0, pl.ds(8, 8), :] = lax.fori_loop(0, 16, lambda r, t: squares(go, 2 * r + c, t), zero)
     norm_push(0)
+    norm_take(0)
+    norm_push(1)
     far(1)
     direct(1, 1)
-    norm_take(0)
-    norm_push(1)
     hand_over(1)
     norm_take(1)
     norm_push(2)

time: 131 us -> 129 us (0.985)
  no operation moved by 1% of the time
where the time goes in v8:
time: 129 us; the launch traced here: 128 us
  Pallas kernels  127 us (98%)
    pallas_call x1, Pallas kernels, shards(): pl.pallas_call(kernel, name='block', out_shape=(jax.ShapeDtypeStruct((row...  125 us

profile of v8, /device:TPU:32, one launch (start us, length us, event | category | flops | bytes accessed | tf_op | source)
XLA Modules:
  0.0 128.0 jit_solution(7823523908864145010)
XLA Ops:
  0.6 125.2 %block.1 = (bf16[512,768]{1,0:T(8,128)(2,1)}, f32[2]{0:T(128)}) custom-call(bf16[512,768]{1,0:T(8,128)(2,1)} %x_ref.1, f32[6144]{0:T(1024)} %gain_ref.1, f32[128]{0:T(128)} %qg_ref.1, f32[128]{0:T(128)} %kg_ref.1, bf16[3,192,384]{2,1,0:T(8,128)(2,1)} %bitcast.1, bf16[192,384]{1,0:T(8,128)(2,1)} %wo_ref.1), custom_call_target="tpu_custom_call" | custom-call | tf_op jit(solution)/shard_map/block/pallas_call | solution.py:664
  125.8 2.0 %deliver.1 = (bf16[512,768]{1,0:T(8,128)(2,1)}, f32[2]{0:T(128)}) custom-call(bf16[512,768]{1,0:T(8,128)(2,1)} %get-tuple-element.4.out_ref, f32[2]{0:T(128)} %get-tuple-element.5.norm_ref), custom_call_target="tpu_custom_call" | custom-call | tf_op jit(solution)/shard_map/deliver/pallas_call | solution.py:702
